TPU v7x, 512 devices: a whole 4x8x8 slice. The times are simulated.
512 devices in a mesh: dp: 32 (over z, y_hi), tensor: 16 (over x, y_lo, core).
Axes of the slice: x: 4, y: 8 (y_hi: 4, y_lo: 2; y = y_hi * 2 + y_lo), z: 8, core: 2. Of those that a mesh axis runs over, the one named last changes fastest.
Arguments:
- tokens_in: bfloat16 [4096, 4096], P(('dp', 'tensor')), may hold values from -6 to 6
- grad_out: bfloat16 [4096, 4096], P(('dp', 'tensor')), may hold values from -6 to 6
- gate_pre: bfloat16 [4096, 7168], P('dp', 'tensor'), may hold values from -6 to 6
- up_pre: bfloat16 [4096, 7168], P('dp', 'tensor'), may hold values from -6 to 6
- gate_weight: bfloat16 [4096, 7168], P('dp', 'tensor'), may hold values from -0.09375 to 0.09375
- up_weight: bfloat16 [4096, 7168], P('dp', 'tensor'), may hold values from -0.09375 to 0.09375
- down_weight: bfloat16 [7168, 4096], P('tensor', 'dp'), may hold values from -0.0625 to 0.0625
- norm_gain: float32 [4096], replicated, may hold values from 0.1 to 1.9
Outputs:
- input_grad: bfloat16 [4096, 4096], P(('dp', 'tensor'))
- gain_grad: float32 [4096], replicated
- down_grad: bfloat16 [7168, 4096], P('tensor', 'dp')
All inputs are finite; a program needn't handle non-finite values.
Results may differ from a plain program's by a relative error of at most 0.015.
Values may be sent and summed in bfloat16 or wider, within the bound.
A program may use at most 64 MiB of HBM per device.

v0:
```python
import functools

import jax
import jax.numpy as jnp
from jax import lax
from jax.sharding import Mesh
from jax.sharding import PartitionSpec as P

TENSOR = ("tensor_0", "tensor_1", "tensor_2")
DP = ("dp_0", "dp_1")
DP_TENSOR = ("dp_0", "dp_1", "tensor_0", "tensor_1", "tensor_2")


def joined_along(tiles, dim):
    dims = list(tiles.shape[1:])
    dims[dim] *= tiles.shape[0]
    return jnp.moveaxis(tiles, 0, dim).reshape(dims)


def sent_to_all(x, axis):
    copies = jnp.broadcast_to(x, (lax.axis_size(axis), *x.shape))
    return lax.all_to_all(copies, axis, split_axis=0, concat_axis=0, tiled=True)


def collect(x, axis, dim):
    return joined_along(sent_to_all(x, axis), dim)


def gathered_by_axis(x, axes, dim):
    filled = x
    for number in range(len(axes) - 1, -1, -1):
        filled = lax.all_gather(filled, axes[number], axis=dim, tiled=True)
    return filled


def sent_together(arrays, axis, dim, along):
    both = jnp.concatenate(arrays, axis=along)
    filled, at, done = (lax.all_gather(both, axis, axis=dim, tiled=True), 0, [])
    for a in arrays:
        done.append(lax.slice_in_dim(filled, at, at + a.shape[along], axis=along))
        at += a.shape[along]
    return tuple(done)


def split_up(x, dim, size):
    dims = x.shape
    tiles = x.reshape(*dims[:dim], size, dims[dim] // size, *dims[dim + 1 :])
    return jnp.moveaxis(tiles, dim, 0)


def sum_at_owner(x, axis, dim):
    tiles = split_up(x, dim, lax.axis_size(axis))
    arrived = lax.all_to_all(tiles, axis, split_axis=0, concat_axis=0, tiled=True)
    return arrived.astype(jnp.float32).sum(axis=0)


def by_axis(x, axes):
    return functools.reduce(lax.psum, axes, x)


def per_device(
    tokens_in, grad_out, gate_pre, up_pre, gate_weight, up_weight, down_weight, norm_gain
):
    group_out = collect(grad_out, TENSOR, 0)
    gate_value = gate_pre.astype(jnp.float32)
    up_value = up_pre.astype(jnp.float32)
    gate_sigmoid = jax.nn.sigmoid(gate_value)
    gate_silu = gate_value * gate_sigmoid
    act = (gate_silu * up_value).astype(jnp.bfloat16)
    grad_act = lax.dot_general(
        group_out,
        lax.all_gather(down_weight, DP, axis=1, tiled=True),
        (((1,), (1,)), ((), ())),
        preferred_element_type=jnp.float32,
    )
    grad_gate = (
        grad_act * up_value * gate_sigmoid * (1.0 + gate_value * (1.0 - gate_sigmoid))
    ).astype(jnp.bfloat16)
    grad_up = (grad_act * gate_silu).astype(jnp.bfloat16)
    pieces = sent_together((gate_weight, up_weight), DP, 0, 1)
    part = lax.dot_general(
        grad_gate, pieces[0], (((1,), (1,)), ((), ())), preferred_element_type=jnp.float32
    )
    part = part + lax.dot_general(
        grad_up, pieces[1], (((1,), (1,)), ((), ())), preferred_element_type=jnp.float32
    )
    grad_norm = sum_at_owner(part.astype(jnp.bfloat16), TENSOR, 0)
    every_out = lax.all_to_all(group_out, DP, split_axis=1, concat_axis=0, tiled=True)
    total = lax.dot_general(
        gathered_by_axis(act, DP, 0),
        every_out,
        (((0,), (0,)), ((), ())),
        preferred_element_type=jnp.float32,
    )
    down_grad = total.astype(jnp.bfloat16)
    inputs = tokens_in.astype(jnp.float32)
    inv_rms = lax.rsqrt(jnp.mean(inputs * inputs, axis=1, keepdims=True) + 1e-05)
    normed = inputs * inv_rms
    gain_grad = by_axis(jnp.sum(grad_norm * normed, axis=0), DP_TENSOR)
    scaled = grad_norm * norm_gain
    inner = jnp.mean(scaled * normed, axis=1, keepdims=True)
    input_grad = (grad_out.astype(jnp.float32) + inv_rms * (scaled - normed * inner)).astype(
        jnp.bfloat16
    )
    return (input_grad, gain_grad, down_grad)


def solution(mesh):
    finer = Mesh(
        mesh.devices.reshape(8, 4, 4, 2, 2), ("dp_0", "dp_1", "tensor_0", "tensor_1", "tensor_2")
    )
    return jax.shard_map(
        per_device,
        mesh=finer,
        in_specs=(
            P(DP_TENSOR, None),
            P(DP_TENSOR, None),
            P(DP, TENSOR),
            P(DP, TENSOR),
            P(DP, TENSOR),
            P(DP, TENSOR),
            P(TENSOR, DP),
            P(),
        ),
        out_specs=(P(DP_TENSOR, None), P(), P(TENSOR, DP)),
        check_vma=False,
    )
```

profile of v0, /device:TPU:1, one launch (start us, length us, event | category | flops | bytes accessed | tf_op | source)
XLA Modules:
  0.0 410.2 jit_solution(10358685831933093235)
XLA Ops:
  7.2 0.0 all-gather.4.cloned.1.call-start
  7.2 0.7 all-gather.4.cloned.1.call-update
  7.9 0.0 all-gather.6.cloned.1.call-start
  7.9 1.7 pad_maximum_fusion
  9.6 0.0 all-gather.6.cloned.1.call-update
  9.6 0.0 all-gather.8.cloned.1.call-start
  9.7 1.0 fusion.10
  10.7 20.8 %all_gather.14 = bf16[512,448]{0,1:T(8,128)(2,1)} all-gather(bf16[128,448]{0,1:T(8,128)(2,1)S(1)} %fusion.10), channel_id=1, replica_groups=mesh['dp_0'=8,'dp_1'=4,'tensor_0'=4,'tensor_1'=2,'tensor_2'=2] {'dp_1'}, dimensions={0}, use_global_device_ids=true | all-gather | bytes 573440 | tf_op jit(solution)/shard_map/all_gather | solution.py:32
  31.5 0.0 all-gather.8.cloned.1.call-update
  31.5 0.9 broadcast_in_dim.2
  32.5 25.2 %all_to_all.29 = bf16[16,8,4096]{2,1,0:T(8,128)(2,1)S(1)} all-to-all(bf16[16,8,4096]{2,1,0:T(8,128)(2,1)S(1)} %broadcast_in_dim.2), channel_id=1, replica_groups=mesh['dp_0'=8,'dp_1'=4,'tensor_0'=4,'tensor_1'=2,'tensor_2'=2] {'tensor_..., dimensions={0} | all-to-all | bytes 2097152 | tf_op jit(solution)/shard_map/all_to_all | solution.py:22
  57.7 0.2 copy.13
  57.9 1.4 copy.12
  59.3 0.0 copy-start
  59.3 0.0 copy-start.2
  59.3 12.6 %all-to-all-start.2 = ((bf16[128,32,128]{2,0,1:T(8,128)(2,1)}), bf16[128,32,128]{2,0,1:T(8,128)(2,1)S(1)}, u32[]{:S(2)}, u32[]{:S(2)}) async-start(bf16[128,32,128]{2,0,1:T(8,128)(2,1)} %copy.12), calls=%async_computation.2 | async-start | bytes 2097152 | tf_op jit(solution)/shard_map/all_to_all | solution.py:88
  71.9 58.1 %all-gather.4.cloned.1.call-done = bf16[448,4096]{1,0:T(8,128)(2,1)} async-done(((bf16[448,128]{1,0:T(8,128)(2,1)}), bf16[448,4096]{1,0:T(8,128)(2,1)}) %all-gather.4.cloned.1.call-update) | async-done | bytes 3670032 | tf_op jit(solution)/shard_map/all_gather | solution.py:72
  130.0 3.2 fusion.5
  133.2 125.7 %all-gather.6.cloned.1.call-done = bf16[4096,896]{0,1:T(8,128)(2,1)} async-done(((bf16[128,896]{0,1:T(8,128)(2,1)}), bf16[4096,896]{0,1:T(8,128)(2,1)}) %all-gather.6.cloned.1.call-update) | async-done | bytes 7340048 | tf_op jit(solution)/shard_map/all_gather | solution.py:38
  258.9 0.0 copy-done
  258.9 0.0 copy-done.2
  258.9 2.8 fusion.3
  261.7 0.0 copy-start.1
  261.7 3.9 fusion.1
  265.6 0.0 all-to-all-done.2
  265.6 18.0 %all-to-all-start.1 = ((bf16[16,8,4096]{2,1,0:T(8,128)(2,1)}), bf16[16,8,4096]{2,1,0:T(8,128)(2,1)S(1)}, u32[]{:S(2)}, u32[]{:S(2)}) async-start(bf16[16,8,4096]{2,1,0:T(8,128)(2,1)} %fusion.1), calls=%async_computation.1 | async-start | bytes 2097152 | tf_op jit(solution)/shard_map/all_to_all | solution.py:53
  283.6 0.0 copy-done.1
  283.6 0.0 copy-start.4
  283.6 0.0 copy-start.3
  283.6 0.1 fusion.24
  283.8 38.5 %all-gather.8.cloned.1.call-done = bf16[4096,448]{0,1:T(8,128)(2,1)} async-done(((bf16[512,448]{0,1:T(8,128)(2,1)}), bf16[4096,448]{0,1:T(8,128)(2,1)}) %all-gather.8.cloned.1.call-update) | async-done | bytes 3670032 | tf_op jit(solution)/shard_map/all_gather | solution.py:32
  322.3 3.8 convolution_convert_fusion
  326.1 0.0 all-to-all-done.1
  326.1 0.1 convert_reduce_fusion
  326.2 0.0 copy-done.4
  326.3 0.2 fusion.23
  326.5 0.0 copy-done.3
  326.5 0.7 fusion.22
  327.2 20.9 %psum.35 = f32[4096]{0:T(1024)S(1)} all-reduce(f32[4096]{0:T(1024)S(1)} %get-tuple-element.3), channel_id=1, replica_groups=mesh['dp_0'=8,'dp_1'=4,'tensor_0'=4,'tensor_1'=2,'tensor_2'=2] {'dp_0'}, use_global_device_ids=true, to_apply=%region_4.0 | all-reduce | flops 4096 | bytes 32768 | tf_op jit(solution)/shard_map/psum | solution.py:58
  348.1 15.9 %psum.36 = f32[4096]{0:T(1024)S(1)} all-reduce(f32[4096]{0:T(1024)S(1)} %psum.35), channel_id=1, replica_groups=mesh['dp_0'=8,'dp_1'=4,'tensor_0'=4,'tensor_1'=2,'tensor_2'=2] {'dp_1'}, use_global_device_ids=true, to_apply=%region_5.0 | all-reduce | flops 4096 | bytes 32768 | tf_op jit(solution)/shard_map/psum | solution.py:58
  364.1 13.0 %psum.37 = f32[4096]{0:T(1024)S(1)} all-reduce(f32[4096]{0:T(1024)S(1)} %psum.36), channel_id=1, replica_groups=mesh['dp_0'=8,'dp_1'=4,'tensor_0'=4,'tensor_1'=2,'tensor_2'=2] {'tensor_0'}, use_global_device_ids=true, to_apply=%region_6.0 | all-reduce | flops 4096 | bytes 32768 | tf_op jit(solution)/shard_map/psum | solution.py:58
  377.1 5.2 %psum.38 = f32[4096]{0:T(1024)S(1)} all-reduce(f32[4096]{0:T(1024)S(1)} %psum.37), channel_id=1, replica_groups=mesh['dp_0'=8,'dp_1'=4,'tensor_0'=4,'tensor_1'=2,'tensor_2'=2] {'tensor_1'}, use_global_device_ids=true, to_apply=%region_7.0 | all-reduce | flops 4096 | bytes 32768 | tf_op jit(solution)/shard_map/psum | solution.py:58
  382.3 21.4 %psum.39 = f32[4096]{0:T(1024)} all-reduce(f32[4096]{0:T(1024)S(1)} %psum.38), channel_id=1, replica_groups=mesh['dp_0'=8,'dp_1'=4,'tensor_0'=4,'tensor_1'=2,'tensor_2'=2] {'tensor_2'}, use_global_device_ids=true, to_apply=%region_8.0 | all-reduce | flops 4096 | bytes 32768 | tf_op jit(solution)/shard_map/psum | solution.py:58
  (2 shorter events, 0.0 us)
Async XLA Ops:
  7.2 122.9 %all-gather.4.cloned.1.call-start = ((), (), s32[]{:S(2)}) async-start(), calls=%async_computation.3 | async-start | bytes 3784704 | tf_op jit(solution)/shard_map/all_gather | solution.py:72
  7.9 251.0 %all-gather.6.cloned.1.call-start = ((), (), s32[]{:S(2)}) async-start(), calls=%async_computation.4 | async-start | bytes 7569408 | tf_op jit(solution)/shard_map/all_gather | solution.py:38
  9.6 312.7 %all-gather.8.cloned.1.call-start = ((), (), s32[]{:S(2)}) async-start(), calls=%async_computation.5 | async-start | bytes 4128768 | tf_op jit(solution)/shard_map/all_gather | solution.py:32
  59.3 199.5 %copy-start = (bf16[128,448]{0,1:T(8,128)(2,1)S(1)}, bf16[128,448]{0,1:T(8,128)(2,1)}, u32[]{:S(2)}) copy-start(bf16[128,448]{0,1:T(8,128)(2,1)} %param.10) | copy-start | bytes 344068
  59.3 199.5 %copy-start.2 = (bf16[128,448]{0,1:T(8,128)(2,1)S(1)}, bf16[128,448]{0,1:T(8,128)(2,1)}, u32[]{:S(2)}) copy-start(bf16[128,448]{0,1:T(8,128)(2,1)} %param.11) | copy-start | bytes 344068
  59.3 206.3 %all-to-all-start.2 = ((bf16[128,32,128]{2,0,1:T(8,128)(2,1)}), bf16[128,32,128]{2,0,1:T(8,128)(2,1)S(1)}, u32[]{:S(2)}, u32[]{:S(2)}) async-start(bf16[128,32,128]{2,0,1:T(8,128)(2,1)} %copy.12), calls=%async_computation.2 | async-start | bytes 2097152 | tf_op jit(solution)/shard_map/all_to_all | solution.py:88
  261.7 21.9 %copy-start.1 = (bf16[8,4096]{1,0:T(8,128)(2,1)S(1)}, bf16[8,4096]{1,0:T(8,128)(2,1)}, u32[]{:S(2)}) copy-start(bf16[8,4096]{1,0:T(8,128)(2,1)} %param.8) | copy-start | bytes 196612
  265.6 60.5 %all-to-all-start.1 = ((bf16[16,8,4096]{2,1,0:T(8,128)(2,1)}), bf16[16,8,4096]{2,1,0:T(8,128)(2,1)S(1)}, u32[]{:S(2)}, u32[]{:S(2)}) async-start(bf16[16,8,4096]{2,1,0:T(8,128)(2,1)} %fusion.1), calls=%async_computation.1 | async-start | bytes 2097152 | tf_op jit(solution)/shard_map/all_to_all | solution.py:53
  283.6 42.7 %copy-start.4 = (f32[4096]{0:T(1024)S(1)}, f32[4096]{0:T(1024)}, u32[]{:S(2)}) copy-start(f32[4096]{0:T(1024)} %param.15) | copy-start | bytes 49156
  283.6 42.9 %copy-start.3 = (bf16[8,4096]{1,0:T(8,128)(2,1)S(1)}, bf16[8,4096]{1,0:T(8,128)(2,1)}, u32[]{:S(2)}) copy-start(bf16[8,4096]{1,0:T(8,128)(2,1)} %param.9) | copy-start | bytes 196612
Sparse Core Ops, SparseCore 0:
  11.0 118.9 all-gather.3
  133.1 125.7 all-gather.5
  260.9 61.3 all-gather.7
where the time goes:
time: 411 us; the launch traced here: 410 us
  waiting for transfers between devices  223 us (54%)
  blocking collectives  122 us (30%)
  starting transfers between devices  30.7 us (7%)
  between operations  13.8 us (3%)
  matrix products  13.7 us (3%)
    all_gather x1, waiting for transfers between devices, sent_together(): filled, at, done = (lax.all_gather(both, axis, axis=dim, tiled=True), 0, [])  126 us
    psum x5, blocking collectives, by_axis(): return functools.reduce(lax.psum, axes, x)  76.5 us
    all_gather x1, waiting for transfers between devices, per_device(): lax.all_gather(down_weight, DP, axis=1, tiled=True)  58.1 us
    all_gather x1, waiting for transfers between devices, gathered_by_axis(): filled = lax.all_gather(filled, axes[number], axis=dim, tiled=True)  38.5 us
    all_to_all x1, blocking collectives, sent_to_all(): return lax.all_to_all(copies, axis, split_axis=0, concat_axis=0, tiled=True)  25.2 us
    all_gather x1, blocking collectives, gathered_by_axis(): filled = lax.all_gather(filled, axes[number], axis=dim, tiled=True)  20.8 us
    all_to_all x1, starting transfers between devices, sum_at_owner(): lax.all_to_all(tiles, axis, split_axis=0, concat_axis=0, tiled=True)  18 us
    all_to_all x1, starting transfers between devices, per_device(): lax.all_to_all(group_out, DP, split_axis=1, concat_axis=0, tiled=True)  12.6 us
  transfers between devices with their start and end apart: 5, of which 3 were waited for; matrix products, arithmetic and copies ran while one was open for 5% of the time, Pallas kernels for 0%

commit v1 on v0

v1 whole, which is shorter than its diff:
```python
import jax
import jax.numpy as jnp
from jax import lax
from jax.sharding import Mesh
from jax.sharding import PartitionSpec as P

Z = "dp_0"
YH = "dp_1"
TENSOR = ("tensor_0", "tensor_1", "tensor_2")
DP = ("dp_0", "dp_1")
DP_TENSOR = ("dp_0", "dp_1", "tensor_0", "tensor_1", "tensor_2")


def nt(a, b):
    return lax.dot_general(a, b, (((1,), (1,)), ((), ())), preferred_element_type=jnp.float32)


def tn(a, b):
    return lax.dot_general(a, b, (((0,), (0,)), ((), ())), preferred_element_type=jnp.float32)


def swap(x, axis):
    return lax.all_to_all(x, axis, split_axis=0, concat_axis=0, tiled=True)


def per_device(
    tokens_in, grad_out, gate_pre, up_pre, gate_weight, up_weight, down_weight, norm_gain
):
    mine = swap(grad_out.reshape(8, 8, 4, 128).transpose(2, 0, 1, 3), YH)
    rows = lax.all_gather(mine.reshape(32, 1024), TENSOR, axis=0, tiled=True)
    rows = rows.reshape(16, 4, 8, 1024).transpose(1, 0, 2, 3).reshape(512, 1024)
    down = lax.all_gather(down_weight, Z, axis=1, tiled=True)
    gate_w = lax.all_gather(gate_weight, Z, axis=0, tiled=True)
    up_w = lax.all_gather(up_weight, Z, axis=0, tiled=True)
    gate = lax.all_gather(gate_pre, YH, axis=0, tiled=True).astype(jnp.float32)
    up = lax.all_gather(up_pre, YH, axis=0, tiled=True).astype(jnp.float32)
    sig = jax.nn.sigmoid(gate)
    silu = gate * sig
    act = (silu * up).astype(jnp.bfloat16)
    part = nt(rows, down).astype(jnp.bfloat16).reshape(4, 128, 448)
    grad_act = swap(part, YH).astype(jnp.float32).sum(axis=0).astype(jnp.bfloat16)
    grad_act = lax.all_gather(grad_act, YH, axis=0, tiled=True).astype(jnp.float32)
    grad_gate = (grad_act * up * sig * (1.0 + gate * (1.0 - sig))).astype(jnp.bfloat16)
    grad_up = (grad_act * silu).astype(jnp.bfloat16)
    norm = (nt(grad_gate, gate_w) + nt(grad_up, up_w)).astype(jnp.bfloat16)
    norm = norm.reshape(4, 16, 8, 1024).transpose(1, 0, 2, 3)
    norm = swap(norm, TENSOR).astype(jnp.float32).sum(axis=0)
    norm = swap(norm, YH).reshape(4, 8, 8, 128)
    grad_norm = norm.transpose(1, 2, 0, 3).reshape(8, 4096)
    total = tn(act, rows).astype(jnp.bfloat16).reshape(448, 8, 128).transpose(1, 0, 2)
    down_grad = swap(total, Z).astype(jnp.float32).sum(axis=0).astype(jnp.bfloat16)

    inputs = tokens_in.astype(jnp.float32)
    inv_rms = lax.rsqrt(jnp.mean(inputs * inputs, axis=1, keepdims=True) + 1e-05)
    normed = inputs * inv_rms
    gain_grad = lax.psum(jnp.sum(grad_norm * normed, axis=0), DP_TENSOR)
    scaled = grad_norm * norm_gain
    inner = jnp.mean(scaled * normed, axis=1, keepdims=True)
    input_grad = (grad_out.astype(jnp.float32) + inv_rms * (scaled - normed * inner)).astype(
        jnp.bfloat16
    )
    return (input_grad, gain_grad, down_grad)


def solution(mesh):
    finer = Mesh(
        mesh.devices.reshape(8, 4, 4, 2, 2), ("dp_0", "dp_1", "tensor_0", "tensor_1", "tensor_2")
    )
    return jax.shard_map(
        per_device,
        mesh=finer,
        in_specs=(
            P(DP_TENSOR, None),
            P(DP_TENSOR, None),
            P(DP, TENSOR),
            P(DP, TENSOR),
            P(DP, TENSOR),
            P(DP, TENSOR),
            P(TENSOR, DP),
            P(),
        ),
        out_specs=(P(DP_TENSOR, None), P(), P(TENSOR, DP)),
        check_vma=False,
    )
```

time: 411 us -> 347 us (0.84)
  waiting for transfers between devices: 223 us -> 45.7 us
  blocking collectives: 122 us -> 236 us
  matrix products: 13.7 us -> 3.15 us
  starting transfers between devices: 30.7 us -> 37.8 us
    all_gather x3 -> x1, waiting for transfers between devices: 222 us -> 0.01 us  [per_device(): rows = lax.all_gather(mine.reshape(32, 1024), TENSOR, axis=0, tiled=True)]
    all_gather x1 -> x6, blocking collectives: 20.8 us -> 127 us  [the longest x1 28.1 us: per_device(): gate_w = lax.all_gather(gate_weight, Z, axis=0, tiled=True)]
    all_to_all x2 -> x4, waiting for transfers between devices: 0.01 us -> 45.7 us  [swap(): return lax.all_to_all(x, axis, split_axis=0, concat_axis=0, tiled=True)]
    psum x5 -> x1, blocking collectives: 76.5 us -> 95.1 us  [per_device(): gain_grad = lax.psum(jnp.sum(grad_norm * normed, axis=0), DP_TENSOR)]
    all_to_all x1, blocking collectives: 25.2 us -> 14.3 us  [swap(): return lax.all_to_all(x, axis, split_axis=0, concat_axis=0, tiled=True)]
    dot_general x4, matrix products: 13.7 us -> 3.15 us  [the longest x3 2.43 us: nt(): lax.dot_general(a, b, (((1,), (1,)), ((), ())), preferred_element_type=jn...]
    all_to_all x2 -> x4, starting transfers between devices: 30.6 us -> 37.8 us  [swap(): return lax.all_to_all(x, axis, split_axis=0, concat_axis=0, tiled=True)]
    reshape x0 -> x6, local copies, waits for them, and re-layouts: none -> 5.29 us  [the longest x1 1.31 us: per_device(): rows = rows.reshape(16, 4, 8, 1024).transpose(1, 0, 2, 3).reshape(512, 1024)]
  transfers between devices with their start and end apart: 5 -> 5, of which waited for: 3 -> 3; matrix products, arithmetic and copies ran while one was open for 5% -> 1% of each run, Pallas kernels for 0% -> 0%
where the time goes in v1:
time: 347 us; the launch traced here: 346 us
  blocking collectives  236 us (68%)
  waiting for transfers between devices  45.7 us (13%)
  starting transfers between devices  37.8 us (11%)
  between operations  14.2 us (4%)
  local copies, waits for them, and re-layouts  6.3 us (2%)
    psum x1, blocking collectives, per_device(): gain_grad = lax.psum(jnp.sum(grad_norm * normed, axis=0), DP_TENSOR)  95.1 us
    all_to_all x4, waiting for transfers between devices, swap(): return lax.all_to_all(x, axis, split_axis=0, concat_axis=0, tiled=True)  45.7 us
    all_to_all x4, starting transfers between devices, swap(): return lax.all_to_all(x, axis, split_axis=0, concat_axis=0, tiled=True)  37.8 us
    all_gather x1, blocking collectives, per_device(): gate_w = lax.all_gather(gate_weight, Z, axis=0, tiled=True)  28.1 us
    all_gather x1, blocking collectives, per_device(): gate = lax.all_gather(gate_pre, YH, axis=0, tiled=True).astype(jnp.float32)  23.9 us
    all_gather x1, blocking collectives, per_device(): down = lax.all_gather(down_weight, Z, axis=1, tiled=True)  22.6 us
    all_gather x1, blocking collectives, per_device(): up_w = lax.all_gather(up_weight, Z, axis=0, tiled=True)  20.3 us
    all_gather x1, blocking collectives, per_device(): lax.all_gather(grad_act, YH, axis=0, tiled=True).astype(jnp.float32)  16.1 us
  transfers between devices with their start and end apart: 5, of which 3 were waited for; matrix products, arithmetic and copies ran while one was open for 1% of the time, Pallas kernels for 0%

profile of v1, /device:TPU:1, one launch (start us, length us, event | category | flops | bytes accessed | tf_op | source)
XLA Modules:
  0.0 346.4 jit_solution(479711068150174751)
XLA Ops:
  7.2 0.0 all-gather.2.cloned.1.call-start
  7.2 0.9 copy.37
  8.1 14.3 %all_to_all.25 = bf16[4,8,8,128]{3,2,1,0:T(8,128)(2,1)S(1)} all-to-all(bf16[4,8,8,128]{3,2,1,0:T(8,128)(2,1)S(1)} %bitcast.51), channel_id=1, replica_groups=mesh['dp_0'=8,'dp_1'=4,'tensor_0'=4,'tensor_1'=2,'tensor_2'=2] {'dp_1'}, dimensions={0} | all-to-all | bytes 131072 | tf_op jit(solution)/shard_map/all_to_all | solution.py:23
  22.4 0.6 copy.36
  23.0 0.0 all-gather.2.cloned.1.call-update
  23.1 28.1 %all_gather.26 = bf16[1024,448]{0,1:T(8,128)(2,1)S(1)} all-gather(bf16[128,448]{0,1:T(8,128)(2,1)} %param.12), channel_id=1, replica_groups=mesh['dp_0'=8,'dp_1'=4,'tensor_0'=4,'tensor_1'=2,'tensor_2'=2] {'dp_0'}, dimensions={0}, use_global_device_ids=true | all-gather | bytes 1032192 | tf_op jit(solution)/shard_map/all_gather | solution.py:33
  51.2 22.6 %all_gather.22 = bf16[448,1024]{1,0:T(8,128)(2,1)S(1)} all-gather(bf16[448,128]{1,0:T(8,128)(2,1)} %param.14), channel_id=1, replica_groups=mesh['dp_0'=8,'dp_1'=4,'tensor_0'=4,'tensor_1'=2,'tensor_2'=2] {'dp_0'}, dimensions={1}, use_global_device_ids=true | all-gather | bytes 1032192 | tf_op jit(solution)/shard_map/all_gather | solution.py:32
  73.7 0.0 all-gather.2.cloned.1.call-done
  73.7 1.3 copy.17
  75.1 0.0 copy-start.5
  75.1 0.7 fusion.1
  75.7 0.0 copy-start.6
  75.8 0.8 copy.34
  76.6 3.5 all-to-all-start.1
  80.1 0.0 copy-done.5
  80.1 23.9 %all_gather.25 = bf16[512,448]{0,1:T(8,128)(2,1)S(1)} all-gather(bf16[128,448]{0,1:T(8,128)(2,1)S(1)} %copy-done.5), channel_id=1, replica_groups=mesh['dp_0'=8,'dp_1'=4,'tensor_0'=4,'tensor_1'=2,'tensor_2'=2] {'dp_1'}, dimensions={0}, use_global_device_ids=true | all-gather | bytes 573440 | tf_op jit(solution)/shard_map/all_gather | solution.py:35
  104.0 0.0 copy-done.6
  104.0 16.0 %all_gather.24 = bf16[512,448]{0,1:T(8,128)(2,1)S(1)} all-gather(bf16[128,448]{0,1:T(8,128)(2,1)S(1)} %copy-done.6), channel_id=1, replica_groups=mesh['dp_0'=8,'dp_1'=4,'tensor_0'=4,'tensor_1'=2,'tensor_2'=2] {'dp_1'}, dimensions={0}, use_global_device_ids=true | all-gather | bytes 573440 | tf_op jit(solution)/shard_map/all_gather | solution.py:36
  120.0 0.0 copy-start.2
  120.0 20.3 %all_gather.27 = bf16[1024,448]{0,1:T(8,128)(2,1)} all-gather(bf16[128,448]{0,1:T(8,128)(2,1)} %param.13), channel_id=1, replica_groups=mesh['dp_0'=8,'dp_1'=4,'tensor_0'=4,'tensor_1'=2,'tensor_2'=2] {'dp_0'}, dimensions={0}, use_global_device_ids=true | all-gather | bytes 1032192 | tf_op jit(solution)/shard_map/all_gather | solution.py:34
  140.4 0.0 all-to-all-done.1
  140.4 0.1 reduce_sum.61
  140.4 16.1 %all_gather.23 = bf16[512,448]{0,1:T(8,128)(2,1)S(1)} all-gather(bf16[128,448]{0,1:T(8,128)(2,1)S(1)} %reduce_sum.61), channel_id=1, replica_groups=mesh['dp_0'=8,'dp_1'=4,'tensor_0'=4,'tensor_1'=2,'tensor_2'=2] {'dp_1'}, dimensions={0}, use_global_device_ids=true | all-gather | bytes 573440 | tf_op jit(solution)/shard_map/all_gather | solution.py:42
  156.6 0.0 copy-start
  156.6 0.9 fusion.11
  157.5 0.0 copy-done.2
  157.5 0.2 copy-done
  157.8 0.8 add_convert_fusion
  158.6 0.0 copy-start.3
  158.6 1.1 copy.32
  159.7 25.8 %all-to-all-start.2 = ((bf16[16,4,8,1024]{3,2,1,0:T(8,128)(2,1)}), bf16[16,4,8,1024]{3,2,1,0:T(8,128)(2,1)S(1)}, u32[]{:S(2)}, u32[]{:S(2)}) async-start(bf16[16,4,8,1024]{3,2,1,0:T(8,128)(2,1)} %bitcast.36), calls=%async_computation.2 | async-start | bytes 2097152 | tf_op jit(solution)/shard_map/all_to_all | solution.py:23
  185.5 0.0 copy-done.3
  185.5 0.7 fusion
  186.2 0.0 copy-start.1
  186.2 1.1 copy.33
  187.4 13.8 %all-to-all-done.2 = bf16[16,4,8,1024]{3,2,1,0:T(8,128)(2,1)S(1)} async-done(((bf16[16,4,8,1024]{3,2,1,0:T(8,128)(2,1)}), bf16[16,4,8,1024]{3,2,1,0:T(8,128)(2,1)S(1)}, u32[]{:S(2)}, u32[]{:S(2)}) %all-to-all-start.2) | async-done | bytes 1048608 | tf_op jit(solution)/shard_map/all_to_all | solution.py:23
  201.1 4.5 %all-to-all-start.4 = ((bf16[8,448,128]{2,1,0:T(8,128)(2,1)}), bf16[8,448,128]{2,1,0:T(8,128)(2,1)S(1)}, u32[]{:S(2)}, u32[]{:S(2)}) async-start(bf16[8,448,128]{2,1,0:T(8,128)(2,1)} %bitcast.38), calls=%async_computation.4 | async-start | bytes 1835008 | tf_op jit(solution)/shard_map/all_to_all | solution.py:23
  205.6 0.0 copy-done.1
  205.6 0.0 copy-start.7
  205.6 0.0 copy-start.4
  205.6 0.1 fusion.25
  205.8 0.8 convert_reduce_fusion
  206.6 25.4 %all-to-all-done.4 = bf16[8,448,128]{2,1,0:T(8,128)(2,1)S(1)} async-done(((bf16[8,448,128]{2,1,0:T(8,128)(2,1)}), bf16[8,448,128]{2,1,0:T(8,128)(2,1)S(1)}, u32[]{:S(2)}, u32[]{:S(2)}) %all-to-all-start.4) | async-done | bytes 917536 | tf_op jit(solution)/shard_map/all_to_all | solution.py:23
  232.0 4.0 %all-to-all-start.3 = ((f32[4,8,1024]{2,1,0:T(8,128)}), f32[4,8,1024]{2,1,0:T(8,128)S(1)}, u32[]{:S(2)}, u32[]{:S(2)}) async-start(f32[4,8,1024]{2,1,0:T(8,128)} %convert_reduce_fusion), calls=%async_computation.3 | async-start | bytes 262144 | tf_op jit(solution)/shard_map/all_to_all | solution.py:23
  236.0 0.8 reduce_sum.65
  236.8 6.6 %all-to-all-done.3 = f32[4,8,1024]{2,1,0:T(8,128)S(1)} async-done(((f32[4,8,1024]{2,1,0:T(8,128)}), f32[4,8,1024]{2,1,0:T(8,128)S(1)}, u32[]{:S(2)}, u32[]{:S(2)}) %all-to-all-start.3) | async-done | bytes 131104 | tf_op jit(solution)/shard_map/all_to_all | solution.py:23
  243.4 0.1 copy.20
  243.5 0.1 reshape.53
  243.5 0.0 copy-done.7
  243.6 0.2 fusion.24
  243.8 95.1 %psum.7 = f32[4096]{0:T(1024)} all-reduce(f32[4096]{0:T(1024)S(1)} %get-tuple-element.3), channel_id=1, replica_groups=mesh['dp_0'=8,'dp_1'=4,'tensor_0'=4,'tensor_1'=2,'tensor_2'=2] {'dp_0','..., use_global_device_ids=true, to_apply=%region_5.0 | all-reduce | flops 4096 | bytes 32768 | tf_op jit(solution)/shard_map/psum | solution.py:56
  338.9 0.0 copy-done.4
  338.9 0.7 fusion.23
  (3 shorter events, 0.0 us)
Async XLA Ops:
  7.2 66.6 %all-gather.2.cloned.1.call-start = ((), (), s32[]{:S(2)}) async-start(), calls=%async_computation.5 | async-start | bytes 1114112 | tf_op jit(solution)/shard_map/all_gather | solution.py:30
  75.1 5.0 %copy-start.5 = (bf16[128,448]{0,1:T(8,128)(2,1)S(1)}, bf16[128,448]{0,1:T(8,128)(2,1)}, u32[]{:S(2)}) copy-start(bf16[128,448]{0,1:T(8,128)(2,1)} %param.10) | copy-start | bytes 344068
  75.7 28.2 %copy-start.6 = (bf16[128,448]{0,1:T(8,128)(2,1)S(1)}, bf16[128,448]{0,1:T(8,128)(2,1)}, u32[]{:S(2)}) copy-start(bf16[128,448]{0,1:T(8,128)(2,1)} %param.11) | copy-start | bytes 344068
  76.6 63.8 %all-to-all-start.1 = ((bf16[4,128,448]{1,2,0:T(8,128)(2,1)}), bf16[4,128,448]{1,2,0:T(8,128)(2,1)S(1)}, u32[]{:S(2)}, u32[]{:S(2)}) async-start(bf16[4,128,448]{1,2,0:T(8,128)(2,1)} %bitcast.39), calls=%async_computation.1 | async-start | bytes 917504 | tf_op jit(solution)/shard_map/all_to_all | solution.py:23
  120.0 37.5 %copy-start.2 = (bf16[512,448]{0,1:T(8,128)(2,1)}, bf16[512,448]{0,1:T(8,128)(2,1)S(1)}, u32[]{:S(2)}) copy-start(bf16[512,448]{0,1:T(8,128)(2,1)S(1)} %all_gather.24) | copy-start | bytes 1376260
  156.6 1.2 copy-start
  158.6 26.9 %copy-start.3 = (bf16[512,448]{0,1:T(8,128)(2,1)S(1)}, bf16[512,448]{0,1:T(8,128)(2,1)}, u32[]{:S(2)}) copy-start(bf16[512,448]{0,1:T(8,128)(2,1)} %copy-done.2) | copy-start | bytes 1376260
  159.7 41.5 %all-to-all-start.2 = ((bf16[16,4,8,1024]{3,2,1,0:T(8,128)(2,1)}), bf16[16,4,8,1024]{3,2,1,0:T(8,128)(2,1)S(1)}, u32[]{:S(2)}, u32[]{:S(2)}) async-start(bf16[16,4,8,1024]{3,2,1,0:T(8,128)(2,1)} %bitcast.36), calls=%async_computation.2 | async-start | bytes 2097152 | tf_op jit(solution)/shard_map/all_to_all | solution.py:23
  186.2 19.4 %copy-start.1 = (bf16[8,4096]{1,0:T(8,128)(2,1)S(1)}, bf16[8,4096]{1,0:T(8,128)(2,1)}, u32[]{:S(2)}) copy-start(bf16[8,4096]{1,0:T(8,128)(2,1)} %param.8) | copy-start | bytes 196612
  201.1 30.9 %all-to-all-start.4 = ((bf16[8,448,128]{2,1,0:T(8,128)(2,1)}), bf16[8,448,128]{2,1,0:T(8,128)(2,1)S(1)}, u32[]{:S(2)}, u32[]{:S(2)}) async-start(bf16[8,448,128]{2,1,0:T(8,128)(2,1)} %bitcast.38), calls=%async_computation.4 | async-start | bytes 1835008 | tf_op jit(solution)/shard_map/all_to_all | solution.py:23
  205.6 37.9 %copy-start.7 = (f32[4096]{0:T(1024)S(1)}, f32[4096]{0:T(1024)}, u32[]{:S(2)}) copy-start(f32[4096]{0:T(1024)} %param.15) | copy-start | bytes 49156
  205.6 133.2 %copy-start.4 = (bf16[8,4096]{1,0:T(8,128)(2,1)S(1)}, bf16[8,4096]{1,0:T(8,128)(2,1)}, u32[]{:S(2)}) copy-start(bf16[8,4096]{1,0:T(8,128)(2,1)} %param.9) | copy-start | bytes 196612
  232.0 11.4 %all-to-all-start.3 = ((f32[4,8,1024]{2,1,0:T(8,128)}), f32[4,8,1024]{2,1,0:T(8,128)S(1)}, u32[]{:S(2)}, u32[]{:S(2)}) async-start(f32[4,8,1024]{2,1,0:T(8,128)} %convert_reduce_fusion), calls=%async_computation.3 | async-start | bytes 262144 | tf_op jit(solution)/shard_map/all_to_all | solution.py:23
Sparse Core Ops, SparseCore 0:
  23.2 39.1 all-gather.1

commit v2 on v1

v2 whole, which is shorter than its diff:
```python
import jax
import jax.numpy as jnp
from jax import lax
from jax.experimental import pallas as pl
from jax.experimental.pallas import tpu as pltpu
from jax.sharding import Mesh
from jax.sharding import PartitionSpec as P

AXES = ("dp_0", "dp_1", "tensor_0", "tensor_1", "tensor_2")
Z, YH, X, YL, C = AXES
TENSOR = AXES[2:]
DP = AXES[:2]
BF = jnp.bfloat16
F32 = jnp.float32
MESH = pl.DeviceIdType.MESH
NZ, NY, NX = 8, 4, 4
N_SEND = 160


def dot(a, b, ca, cb):
    return lax.dot_general(a, b, (((ca,), (cb,)), ((), ())), preferred_element_type=F32)


def kernel(
    tok, gout, gate, up, gw, uw, dw, gain,
    igrad, ggrad, dgrad,
    w, gu, a, st, fac, act, sa, ra, own, ga, pn, rn, qn, rq, fs, fn, ds_, rd, gacc,
    g1, g2, g3, g4, irms,
    ssem, wsem, gsem, s1sem, ylsem, xsem, csem, rasem, gasem, rnsem, rqsem, fnsem, rdsem,
    g1sem, g2sem, g3sem, g4sem,
):
    z, k, x = lax.axis_index(Z), lax.axis_index(YH), lax.axis_index(X)
    yl, c = lax.axis_index(YL), lax.axis_index(C)
    t = x * 4 + yl * 2 + c
    sends = []

    def send(src, dst, dev, rsem):
        cp = pltpu.make_async_remote_copy(
            src_ref=src, dst_ref=dst, send_sem=ssem.at[len(sends)], recv_sem=rsem,
            device_id=dev, device_id_type=MESH,
        )
        cp.start()
        sends.append(cp)

    def arrived(ref, rsem):
        pltpu.make_async_copy(ref, ref, rsem).wait()

    def zz(d):
        return lax.rem(z + d + NZ, NZ)

    def yy(d):
        return lax.rem(k + d + NY, NY)

    def xx(d):
        return lax.rem(x + d, NX)

    xc = [(d, e) for d in range(NX) for e in range(2) if d or e]

    def xc_dev(d, e):
        return {X: xx(d), C: lax.rem(c + e, 2)}

    peers = [{Z: zz(d)} for d in range(1, NZ)] + [{YH: yy(d)} for d in range(1, NY)]
    peers += [xc_dev(d, e) for d, e in xc] + [{YL: 1 - yl}]
    barrier = pltpu.get_barrier_semaphore()
    for p in peers:
        pl.semaphore_signal(barrier, inc=1, device_id=p, device_id_type=MESH)

    for q in range(NY):
        for i in range(NZ):
            col = (i * NY + q) * 128
            st[0, q, :, i * 128:(i + 1) * 128] = gout[:, col:col + 128]
    a[0, k, t] = st[0, k]
    pl.semaphore_wait(barrier, len(peers))

    w_in = (dw, gw, uw)
    gu_in = (gate, up)

    def ring_first(src, buf, me, left, right, sem):
        send(src, buf.at[me], right, sem.at[0, 0])
        send(src, buf.at[me], left, sem.at[1, 0])

    def ring_next(buf, at, s, n, left, right, sem):
        for way, dev in ((0, right), (1, left)):
            slot = buf.at[at(-s if way == 0 else s)]
            arrived(slot, sem.at[way, s - 1])
            if s + 1 < n // 2:
                send(slot, slot, dev, sem.at[way, s])
            else:
                half = slot.at[pl.ds(224 * way, 224)]
                send(half, half, dev, sem.at[way, s])

    def ring_last(buf, at, n, sem):
        slot = buf.at[at(n // 2)]
        for way in range(2):
            arrived(slot.at[pl.ds(224 * way, 224)], sem.at[way, n // 2 - 1])

    zl, zr, yl_, yr_ = {Z: zz(-1)}, {Z: zz(1)}, {YH: yy(-1)}, {YH: yy(1)}

    def w_first(i):
        ring_first(w_in[i], w.at[i], z, zl, zr, wsem.at[i])

    def w_next(i, s):
        ring_next(w.at[i], zz, s, NZ, zl, zr, wsem.at[i])

    def gu_first(i):
        ring_first(gu_in[i], gu.at[i], k, yl_, yr_, gsem.at[i])

    def s1_send(i):
        for d in (2, 1, 3):
            send(st.at[i, yy(d)], a.at[i, k, t], {YH: yy(d)}, s1sem.at[i, d])

    def s1_wait(i):
        for d in (1, 3, 2):
            arrived(a.at[i, yy(-d), t], s1sem.at[i, d])

    def unit(i, t_):
        return a.at[i, :, t_]

    core = {C: 1 - c}
    t_yl = x * 4 + (1 - yl) * 2 + c

    def unit_send(i, j, tj):
        for d in (2, 1, 3):
            send(unit(i, tj), unit(i, tj), {X: xx(d)}, xsem.at[i, j, d])
        send(unit(i, tj), unit(i, tj), core, csem.at[i, 0, j])

    def t_of(d, j):
        return lax.rem(x + NX - d, NX) * 4 + (yl if j == 0 else 1 - yl) * 2 + c

    def unit_x(i, j):
        for d in (1, 3, 2):
            td = t_of(d, j)
            arrived(unit(i, td), xsem.at[i, j, d])
            send(unit(i, td), unit(i, td), core, csem.at[i, d, j])

    def unit_core(i):
        for j in range(2):
            for d in range(NX):
                tc = lax.rem(x + NX - d, NX) * 4 + (yl if j == 0 else 1 - yl) * 2 + 1 - c
                arrived(unit(i, tc), csem.at[i, d, j])

    w_first(0)
    s1_send(0)
    gu_first(0)
    w_first(1)
    gu_first(1)

    tf = tok[...].astype(F32)
    inv = lax.rsqrt(jnp.mean(tf * tf, axis=1, keepdims=True) + 1e-05)
    irms[...] = jnp.broadcast_to(inv, (8, 128))
    for q in range(NY):
        for i in range(NZ):
            col = (i * NY + q) * 128
            st[1, q, :, i * 128:(i + 1) * 128] = (tf[:, col:col + 128] * inv).astype(BF)
    a[1, k, t] = st[1, k]
    for i in range(3):
        w[i, z] = w_in[i][...]
    for i in range(2):
        gu[i, k] = gu_in[i][...]

    s1_wait(0)
    send(unit(0, t), unit(0, t), {YL: 1 - yl}, ylsem.at[0])
    unit_send(0, 0, t)
    w_next(0, 1)
    w_first(2)
    arrived(unit(0, t_yl), ylsem.at[0])
    unit_send(0, 1, t_yl)
    w_next(1, 1)
    w_next(0, 2)
    for i in range(2):
        ring_next(gu.at[i], yy, 1, NY, yl_, yr_, gsem.at[i])
    s1_send(1)
    unit_x(0, 0)
    w_next(2, 1)
    w_next(0, 3)
    unit_x(0, 1)
    w_next(1, 2)
    unit_core(0)
    ring_last(w.at[0], zz, NZ, wsem.at[0])

    down = jnp.concatenate([w[0, i] for i in range(NZ)], axis=1)
    for d in (2, 1, 3, 0):
        rows = a.at[0, yy(d)].reshape(128, 1024)[...]
        part = dot(down, rows, 1, 1)
        if d:
            sa[d] = part.astype(BF)
            send(sa.at[d], ra.at[d], {YH: yy(d)}, rasem.at[d])
        else:
            own[...] = part

    for i in range(2):
        ring_last(gu.at[i], yy, NY, gsem.at[i])
    for j in range(NY):
        gv = gu[0, j].astype(F32)
        uv = gu[1, j].astype(F32)
        sg = jax.nn.sigmoid(gv)
        sv = gv * sg
        fac[0, j] = uv * sg * (1.0 + gv * (1.0 - sg))
        fac[1, j] = sv
        act[j] = (sv * uv).astype(BF)

    w_next(2, 2)
    w_next(1, 3)
    w_next(2, 3)
    s1_wait(1)
    send(unit(1, t), unit(1, t), {YL: 1 - yl}, ylsem.at[1])
    unit_send(1, 0, t)

    for d in (1, 3, 2):
        arrived(ra.at[d], rasem.at[d])
    total = own[...] + ra[1].astype(F32) + ra[2].astype(F32) + ra[3].astype(F32)
    ga[k] = total.astype(BF)
    for d in (2, 1, 3):
        send(ga.at[k], ga.at[k], {YH: yy(d)}, gasem.at[d])

    arrived(unit(1, t_yl), ylsem.at[1])
    unit_send(1, 1, t_yl)
    for i in (1, 2):
        ring_last(w.at[i], zz, NZ, wsem.at[i])

    acts = jnp.concatenate([act[j] for j in range(NY)], axis=1)
    rows_all = a.at[0].reshape(512, 1024)
    for i in range(NZ // 2):
        pair = dot(acts, rows_all[:, i * 256:(i + 1) * 256], 1, 0)
        ds_[2 * i] = pair[:, :128].astype(BF)
        ds_[2 * i + 1] = pair[:, 128:].astype(BF)
    for d in (4, 3, 5, 2, 6, 1, 7):
        send(ds_.at[zz(d)], rd.at[d], {Z: zz(d)}, rdsem.at[d])

    unit_x(1, 0)
    unit_x(1, 1)
    unit_core(1)

    gacc[...] = jnp.zeros((8, 1024), F32)
    for d in (0, 1, 3, 2):
        j = yy(-d)
        if d:
            arrived(ga.at[j], gasem.at[d])
        gj = ga[j].astype(F32)
        both = jnp.concatenate([(gj * fac[0, j]).astype(BF), (gj * fac[1, j]).astype(BF)], axis=0)
        for i in range(NZ // 2):
            cols = jnp.concatenate(
                [
                    jnp.concatenate([w[1, 2 * i], w[2, 2 * i]], axis=0),
                    jnp.concatenate([w[1, 2 * i + 1], w[2, 2 * i + 1]], axis=0),
                ],
                axis=1,
            )
            part = dot(both, cols, 0, 0)
            lanes = slice(i * 256, (i + 1) * 256)
            add = gacc[:, lanes]
            for q in range(16):
                piece = part[q * 8:(q + 1) * 8]
                pn[d, q // 4, (q // 2) % 2, q % 2, :, lanes] = piece.astype(BF)
                add = add + piece * a[1, j, q, :, lanes].astype(F32)
            gacc[:, lanes] = add
        for e, f in sorted(xc, key=lambda v: -min(v[0], 4 - v[0])):
            send(
                pn.at[d, xx(e), :, lax.rem(c + f, 2)], rn.at[d, e * 2 + f],
                xc_dev(e, f), rnsem.at[d, e * 2 + f],
            )

    for i in range(NZ):
        g1[x * 2 + c, i:i + 1, :] = jnp.sum(
            gacc[:, i * 128:(i + 1) * 128], axis=0, keepdims=True
        )
    for e, f in xc:
        send(g1.at[x * 2 + c], g1.at[x * 2 + c], xc_dev(e, f), g1sem.at[e * 2 + f])

    def norm_first(d):
        for e, f in xc:
            arrived(rn.at[d, e * 2 + f], rnsem.at[d, e * 2 + f])
        for_peer = pn[d, x, 1 - yl, c].astype(F32)
        for e, f in xc:
            for_peer = for_peer + rn[d, e * 2 + f, 1 - yl].astype(F32)
        qn[d] = for_peer.astype(BF)
        send(qn.at[d], rq.at[d], {YL: 1 - yl}, rqsem.at[d])

    def norm_second(d):
        mine = pn[d, x, yl, c].astype(F32)
        for e, f in xc:
            mine = mine + rn[d, e * 2 + f, yl].astype(F32)
        arrived(rq.at[d], rqsem.at[d])
        mine = mine + rq[d].astype(F32)
        if d:
            fs[d] = mine
            send(fs.at[d], fn.at[k], {YH: yy(-d)}, fnsem.at[d])
        else:
            fn[k] = mine

    norm_first(1)
    norm_first(3)
    norm_second(1)
    norm_second(3)
    norm_first(2)
    norm_first(0)
    for e, f in xc:
        arrived(g1.at[lax.rem(x + NX - e, NX) * 2 + lax.rem(c + f, 2)], g1sem.at[e * 2 + f])
    g2[yl] = jnp.sum(g1[...], axis=0)
    send(g2.at[yl], g2.at[yl], {YL: 1 - yl}, g2sem.at[0])
    norm_second(2)
    norm_second(0)
    arrived(g2.at[1 - yl], g2sem.at[0])
    g3[z] = g2[0] + g2[1]
    for d in (4, 3, 5, 2, 6, 1, 7):
        send(g3.at[z], g3.at[z], {Z: zz(d)}, g3sem.at[d])

    for d in range(1, NZ):
        arrived(rd.at[d], rdsem.at[d])
    dsum = ds_[z].astype(F32)
    for d in range(1, NZ):
        dsum = dsum + rd[d].astype(F32)
    dgrad[...] = dsum.astype(BF)

    for d in range(1, NZ):
        arrived(g3.at[zz(-d)], g3sem.at[d])
    g4[k] = jnp.sum(g3[...], axis=0)
    for d in (2, 1, 3):
        send(g4.at[k], g4.at[k], {YH: yy(d)}, g4sem.at[d])

    for d in (1, 3, 2):
        arrived(fn.at[yy(d)], fnsem.at[d])
    inv = irms[...]
    inner = jnp.zeros((8, 128), F32)
    for i in range(NZ):
        for q in range(NY):
            b = i * NY + q
            normed = tok[:, b * 128:(b + 1) * 128].astype(F32) * inv
            inner = inner + fn[q, :, i * 128:(i + 1) * 128] * gain[b:b + 1, :] * normed
    inner = jnp.sum(inner, axis=1, keepdims=True) * (1.0 / 4096)
    for i in range(NZ):
        for q in range(NY):
            b = i * NY + q
            cols = slice(b * 128, (b + 1) * 128)
            normed = tok[:, cols].astype(F32) * inv
            scaled = fn[q, :, i * 128:(i + 1) * 128] * gain[b:b + 1, :]
            igrad[:, cols] = (
                gout[:, cols].astype(F32) + inv * (scaled - normed * inner)
            ).astype(BF)

    for d in range(1, NY):
        arrived(g4.at[yy(-d)], g4sem.at[d])
    for i in range(NZ):
        for q in range(NY):
            b = i * NY + q
            ggrad[b:b + 1, :] = g4[q, i:i + 1, :]
    for cp in sends:
        cp.wait_send()


def per_device(
    tokens_in, grad_out, gate_pre, up_pre, gate_weight, up_weight, down_weight, norm_gain
):
    vm = pltpu.VMEM
    dma = pltpu.SemaphoreType.DMA
    scratch = [
        vm((3, NZ, 448, 128), BF),
        vm((2, NY, 448, 128), BF),
        vm((2, NY, 16, 8, 1024), BF),
        vm((2, NY, 8, 1024), BF),
        vm((2, NY, 448, 128), F32),
        vm((NY, 448, 128), BF),
        vm((NY, 448, 128), BF),
        vm((NY, 448, 128), BF),
        vm((448, 128), F32),
        vm((NY, 448, 128), BF),
        vm((NY, NX, 2, 2, 8, 1024), BF),
        vm((NY, 8, 2, 8, 1024), BF),
        vm((NY, 8, 1024), BF),
        vm((NY, 8, 1024), BF),
        vm((NY, 8, 1024), F32),
        vm((NY, 8, 1024), F32),
        vm((NZ, 448, 128), BF),
        vm((NZ, 448, 128), BF),
        vm((8, 1024), F32),
        vm((8, 8, 128), F32),
        vm((2, 8, 128), F32),
        vm((NZ, 8, 128), F32),
        vm((NY, 8, 128), F32),
        vm((8, 128), F32),
        dma((N_SEND,)),
        dma((3, 2, 4)),
        dma((2, 2, 2)),
        dma((2, 4)),
        dma((2,)),
        dma((2, 2, 4)),
        dma((2, 4, 2)),
        dma((4,)),
        dma((4,)),
        dma((4, 8)),
        dma((4,)),
        dma((4,)),
        dma((8,)),
        dma((8,)),
        dma((1,)),
        dma((8,)),
        dma((4,)),
    ]
    spec = pl.BlockSpec(memory_space=pltpu.VMEM)
    igrad, ggrad, dgrad = pl.pallas_call(
        kernel,
        out_shape=(
            jax.ShapeDtypeStruct((8, 4096), BF),
            jax.ShapeDtypeStruct((32, 128), F32),
            jax.ShapeDtypeStruct((448, 128), BF),
        ),
        in_specs=[spec] * 8,
        out_specs=(spec,) * 3,
        scratch_shapes=scratch,
        compiler_params=pltpu.CompilerParams(
            collective_id=0, has_side_effects=True, vmem_limit_bytes=60 * 1024 * 1024
        ),
    )(
        tokens_in, grad_out, gate_pre.T, up_pre.T, gate_weight.T, up_weight.T, down_weight,
        norm_gain.reshape(32, 128),
    )
    return igrad, ggrad.reshape(4096), dgrad


def solution(mesh):
    finer = Mesh(mesh.devices.reshape(NZ, NY, NX, 2, 2), AXES)
    return jax.shard_map(
        per_device,
        mesh=finer,
        in_specs=(
            P(AXES, None),
            P(AXES, None),
            P(DP, TENSOR),
            P(DP, TENSOR),
            P(DP, TENSOR),
            P(DP, TENSOR),
            P(TENSOR, DP),
            P(),
        ),
        out_specs=(P(AXES, None), P(), P(TENSOR, DP)),
        check_vma=False,
    )
```

time: 347 us -> 97.4 us (0.28)
  the two profiles are of different devices: /device:TPU:1 before, /device:TPU:64 now
where the time goes in v2:
time: 97.4 us; the launch traced here: 97.3 us
  Pallas kernels  93.8 us (96%)
  local copies, waits for them, and re-layouts  2.77 us (3%)
    pallas_call x1, Pallas kernels, per_device(): pl.pallas_call(kernel, out_shape=(jax.ShapeDtypeStruct((8, 4096), BF), ja...  93.8 us
    unnamed x7, local copies, waits for them, and re-layouts  2.77 us

profile of v2, /device:TPU:64, one launch (start us, length us, event | category | flops | bytes accessed | tf_op | source)
XLA Modules:
  0.0 97.3 jit_solution(7148185134408162739)
XLA Ops:
  0.6 93.8 %shard_map.103 = (bf16[8,4096]{1,0:T(8,128)(2,1)}, f32[32,128]{1,0:T(8,128)}, bf16[448,128]{1,0:T(8,128)(2,1)}) custom-call(bf16[8,4096]{1,0:T(8,128)(2,1)} %tok.1, bf16[8,4096]{1,0:T(8,128)(2,1)} %gout.1, bf16[448,128]{1,0:T(8,128)(2,1)} %bitcast.6, bf16[448,128]{1,0:T(8,128)(2,1)} %bitcast.7, bf16[448,128]{1,0:T(8,128)(2,1)} %bitcast.8, ...), custom_call_target="tpu_custom_call" | custom-call | tf_op jit(solution)/shard_map/pallas_call | solution.py:400
  94.5 0.0 copy-start
  94.5 0.0 copy-start.1
  94.5 1.5 %copy.14 = bf16[8,4096]{1,0:T(8,128)(2,1)} copy(bf16[8,4096]{1,0:T(8,128)(2,1)} %get-tuple-element.12) | data formatting | bytes 131072
  96.0 0.0 copy-done.1
  96.0 0.6 copy.15
  96.6 0.0 copy-done
  96.6 0.6 copy.16
Async XLA Ops:
  94.5 2.1 %copy-start = (bf16[448,128]{1,0:T(8,128)(2,1)S(1)}, bf16[448,128]{1,0:T(8,128)(2,1)}, u32[]{:S(2)}) copy-start(bf16[448,128]{1,0:T(8,128)(2,1)} %get-tuple-element.14) | copy-start | bytes 344068
  94.5 1.5 %copy-start.1 = (f32[32,128]{1,0:T(8,128)S(1)}, f32[32,128]{1,0:T(8,128)}, u32[]{:S(2)}) copy-start(f32[32,128]{1,0:T(8,128)} %get-tuple-element.7) | copy-start | bytes 49156

commit v3 on v2

v3 whole, which is shorter than its diff:
```python
import jax
import jax.numpy as jnp
from jax import lax
from jax.experimental import pallas as pl
from jax.experimental.pallas import tpu as pltpu
from jax.sharding import Mesh
from jax.sharding import PartitionSpec as P

AXES = ("dp_0", "dp_1", "tensor_0", "tensor_1", "tensor_2")
Z, YH, X, YL, C = AXES
TENSOR = AXES[2:]
DP = AXES[:2]
BF = jnp.bfloat16
F32 = jnp.float32
MESH = pl.DeviceIdType.MESH
NZ, NY, NX = 8, 4, 4
N_SEND = 200


def dot(a, b, ca, cb):
    return lax.dot_general(a, b, (((ca,), (cb,)), ((), ())), preferred_element_type=F32)


def kernel(
    tok_h, gout_h, gate_h, up_h, gw_h, uw_h, dw_h, gain_h,
    igrad, ggrad, dgrad,
    tok, gout, gain,
    w, gu, a, st, fac, act, sa, ra, rb, part, ga, pn, rn, qn, rq, fs, fn, ds_, rd, gacc,
    g1, g2, g3, g4, irms,
    lsem, ssem, wsem, gsem, s1sem, xsem, csem, rasem, rbsem, gasem, rnsem, rqsem, fnsem, rdsem,
    g1sem, g2sem, g3sem, g4sem,
):
    z, k, x = lax.axis_index(Z), lax.axis_index(YH), lax.axis_index(X)
    yl, c = lax.axis_index(YL), lax.axis_index(C)
    sends = []

    def send(src, dst, dev, rsem):
        cp = pltpu.make_async_remote_copy(
            src_ref=src, dst_ref=dst, send_sem=ssem.at[len(sends)], recv_sem=rsem,
            device_id=dev, device_id_type=MESH,
        )
        cp.start()
        sends.append(cp)

    def arrived(ref, rsem):
        pltpu.make_async_copy(ref, ref, rsem).wait()

    def zz(d):
        return lax.rem(z + d + NZ, NZ)

    def yy(d):
        return lax.rem(k + d + NY, NY)

    def xx(d):
        return lax.rem(x + d + NX, NX)

    def ee(v, e):
        return lax.rem(v + e, 2)

    xc = [(d, e) for d in (2, 1, 3, 0) for e in range(2) if d or e]
    ys = [(d, e) for d in (2, 1, 3, 0) for e in (1, 0) if d or e]
    zs = (4, 3, 5, 2, 6, 1, 7)

    def xc_dev(d, e):
        return {X: xx(d), C: ee(c, e)}

    def ys_dev(d, e):
        return {YH: yy(d), YL: ee(yl, e)}

    peers = [{Z: zz(d)} for d in zs]
    peers += [ys_dev(d, e) for d, e in ys] + [xc_dev(d, e) for d, e in xc]
    barrier = pltpu.get_barrier_semaphore()
    for p in peers:
        pl.semaphore_signal(barrier, inc=1, device_id=p, device_id_type=MESH)

    loads = [
        (gout_h, gout), (tok_h, tok), (dw_h, w.at[0, z]), (gate_h, gu.at[0, k]),
        (up_h, gu.at[1, k]), (gw_h, w.at[1, z]), (uw_h, w.at[2, z]), (gain_h, gain),
    ]
    loads = [pltpu.make_async_copy(s, d, lsem.at[i]) for i, (s, d) in enumerate(loads)]
    for cp in loads:
        cp.start()

    loads[0].wait()
    for q in range(NY):
        for i in range(NZ):
            col = (i * NY + q) * 128
            st[0, q, :, i * 128:(i + 1) * 128] = gout[:, col:col + 128]
    a[0, k, x, yl, c] = st[0, k]
    loads[1].wait()
    tf = tok[...].astype(F32)
    inv = lax.rsqrt(jnp.mean(tf * tf, axis=1, keepdims=True) + 1e-05)
    irms[...] = jnp.broadcast_to(inv, (8, 128))
    for q in range(NY):
        for i in range(NZ):
            col = (i * NY + q) * 128
            st[1, q, :, i * 128:(i + 1) * 128] = (tf[:, col:col + 128] * inv).astype(BF)
    a[1, k, x, yl, c] = st[1, k]
    for cp in loads[2:]:
        cp.wait()
    pl.semaphore_wait(barrier, len(peers))

    def half(ref, h):
        return ref.at[pl.ds(224 * h, 224)]

    class Ring:
        def __init__(self, buf, at, me, n, left, right, sem):
            self.buf, self.at, self.me, self.n, self.sem = buf, at, me, n, sem
            self.devs = (right, left)

        def put(self, slot, way, step, h):
            p = half(self.buf.at[slot], h)
            send(p, p, self.devs[way], self.sem.at[way, step, h])

        def first(self):
            for i in range(2):
                for way in range(2):
                    self.put(self.me, way, 0, i ^ way)

        def got(self, s, way, h):
            slot = self.at(-s if way == 0 else s)
            arrived(half(self.buf.at[slot], h), self.sem.at[way, s - 1, h])
            return slot

        def nxt(self, s):
            for i in range(2):
                for way in range(2):
                    slot = self.got(s, way, i ^ way)
                    if s + 1 < self.n // 2 or i == 0:
                        self.put(slot, way, s, i ^ way)

        def last(self):
            for way in range(2):
                self.got(self.n // 2, way, way)

    zl, zr, kl, kr = {Z: zz(-1)}, {Z: zz(1)}, {YH: yy(-1)}, {YH: yy(1)}
    dwr, gwr, uwr = [Ring(w.at[i], zz, z, NZ, zl, zr, wsem.at[i]) for i in range(3)]
    gater, upr = [Ring(gu.at[i], yy, k, NY, kl, kr, gsem.at[i]) for i in range(2)]
    gar = Ring(ga, yy, k, NY, kl, kr, gasem)
    core = {C: 1 - c}

    def s1_send(i):
        for d, e in ys:
            send(st.at[i, yy(d)], a.at[i, k, x, yl, c], ys_dev(d, e), s1sem.at[i, d * 2 + e])

    def s1_wait(i):
        for d, e in reversed(ys):
            arrived(a.at[i, yy(-d), x, ee(yl, e), c], s1sem.at[i, d * 2 + e])

    def unit(i, xs, cs):
        return a.at[i, :, xs, :, cs]

    def x_send(i):
        for d in (2, 1, 3):
            send(unit(i, x, c), unit(i, x, c), {X: xx(d)}, xsem.at[i, d])
        send(unit(i, x, c), unit(i, x, c), core, csem.at[i, 0])

    def x_wait(i):
        for d in (1, 3, 2):
            u = unit(i, xx(-d), c)
            arrived(u, xsem.at[i, d])
            send(u, u, core, csem.at[i, d])

    def core_wait(i):
        for d in (0, 1, 3, 2):
            arrived(unit(i, xx(-d), 1 - c), csem.at[i, d])

    dwr.first()
    s1_send(0)
    gater.first()
    dwr.nxt(1)
    s1_wait(0)
    x_send(0)
    dwr.nxt(2)
    dwr.nxt(3)
    gwr.first()
    gater.nxt(1)
    upr.first()
    uwr.first()
    x_wait(0)
    dwr.last()
    gwr.nxt(1)
    core_wait(0)

    down = jnp.concatenate([w[0, i] for i in range(NZ)], axis=1)

    def partial(d):
        return dot(down, a.at[0, yy(d)].reshape(128, 1024)[...], 1, 1)

    sa[1] = partial(2).astype(BF)
    send(half(sa.at[1], 0), rb.at[0], kr, rbsem.at[0])
    send(half(sa.at[1], 1), rb.at[1], kl, rbsem.at[1])
    for n, (d, dev, h) in enumerate(((1, kr, 1), (3, kl, 0))):
        rows = slice(224 * h, 224 * h + 224)
        part[n] = partial(d)
        sa[2 * n, rows] = part[n, rows].astype(BF)
        send(half(sa.at[2 * n], h), half(ra.at[n], h), dev, rasem.at[n, h])
    part[2] = partial(0)

    uwr.nxt(1)
    upr.nxt(1)
    gwr.nxt(2)

    for n, (dev, h) in enumerate(((kr, 0), (kl, 1))):
        rows = slice(224 * h, 224 * h + 224)
        arrived(rb.at[n], rbsem.at[n])
        sa[2 * n, rows] = (part[n, rows] + rb[n].astype(F32)).astype(BF)
        send(half(sa.at[2 * n], h), half(ra.at[n], h), dev, rasem.at[n, h])
    s1_send(1)

    uwr.nxt(2)

    gater.last()
    upr.last()
    for j in range(NY):
        gv = gu[0, j].astype(F32)
        uv = gu[1, j].astype(F32)
        sg = jax.nn.sigmoid(gv)
        sv = gv * sg
        fac[0, j] = uv * sg * (1.0 + gv * (1.0 - sg))
        fac[1, j] = sv
        act[j] = (sv * uv).astype(BF)
    gwr.nxt(3)

    for n in range(2):
        for h in range(2):
            arrived(half(ra.at[n], h), rasem.at[n, h])
    ga[k] = (part[2] + ra[0].astype(F32) + ra[1].astype(F32)).astype(BF)
    gar.first()

    uwr.nxt(3)
    s1_wait(1)
    x_send(1)
    gwr.last()
    uwr.last()

    def norm_part(d):
        j = yy(-d)
        gj = ga[j].astype(F32)
        both = jnp.concatenate([(gj * fac[0, j]).astype(BF), (gj * fac[1, j]).astype(BF)], axis=0)
        for i in range(NZ // 2):
            cols = jnp.concatenate(
                [
                    jnp.concatenate([w[1, 2 * i], w[2, 2 * i]], axis=0),
                    jnp.concatenate([w[1, 2 * i + 1], w[2, 2 * i + 1]], axis=0),
                ],
                axis=1,
            )
            block = dot(both, cols, 0, 0)
            lanes = slice(i * 256, (i + 1) * 256)
            for q in range(16):
                pn[d, q // 4, (q // 2) % 2, q % 2, :, lanes] = block[q * 8:(q + 1) * 8].astype(BF)
        for e, f in xc:
            send(
                pn.at[d, xx(e), :, ee(c, f)], rn.at[d, e * 2 + f],
                xc_dev(e, f), rnsem.at[d, e * 2 + f],
            )

    def norm_first(d):
        for e, f in reversed(xc):
            arrived(rn.at[d, e * 2 + f], rnsem.at[d, e * 2 + f])
        for_peer = pn[d, x, 1 - yl, c].astype(F32)
        for e, f in xc:
            for_peer = for_peer + rn[d, e * 2 + f, 1 - yl].astype(F32)
        qn[d] = for_peer.astype(BF)
        send(qn.at[d], rq.at[d], {YL: 1 - yl}, rqsem.at[d])

    def norm_second(d):
        mine = pn[d, x, yl, c].astype(F32)
        for e, f in xc:
            mine = mine + rn[d, e * 2 + f, yl].astype(F32)
        arrived(rq.at[d], rqsem.at[d])
        mine = mine + rq[d].astype(F32)
        if d:
            fs[d] = mine
            send(fs.at[d], fn.at[k], {YH: yy(-d)}, fnsem.at[d])
        else:
            fn[k] = mine

    norm_part(0)

    acts = jnp.concatenate([act[j] for j in range(NY)], axis=1)
    rows_all = a.at[0].reshape(512, 1024)
    for i in range(NZ // 2):
        pair = dot(acts, rows_all[:, i * 256:(i + 1) * 256], 1, 0)
        ds_[2 * i] = pair[:, :128].astype(BF)
        ds_[2 * i + 1] = pair[:, 128:].astype(BF)
    for d in zs:
        send(ds_.at[zz(d)], rd.at[d], {Z: zz(d)}, rdsem.at[d])

    gar.nxt(1)
    norm_part(1)
    norm_part(3)
    x_wait(1)
    norm_first(0)
    gar.last()
    norm_part(2)

    core_wait(1)
    add = jnp.zeros((8, 1024), F32)
    for d in range(NY):
        for q in range(16):
            at = (q // 4, (q // 2) % 2, q % 2)
            add = add + pn[(d,) + at].astype(F32) * a[(1, yy(-d)) + at].astype(F32)
    for i in range(NZ):
        g1[x * 2 + c, i:i + 1, :] = jnp.sum(add[:, i * 128:(i + 1) * 128], axis=0, keepdims=True)
    for e, f in xc:
        send(g1.at[x * 2 + c], g1.at[x * 2 + c], xc_dev(e, f), g1sem.at[e * 2 + f])

    norm_second(0)
    norm_first(1)
    norm_first(3)
    for e, f in reversed(xc):
        arrived(g1.at[xx(-e) * 2 + ee(c, f)], g1sem.at[e * 2 + f])
    g2[yl] = jnp.sum(g1[...], axis=0)
    send(g2.at[yl], g2.at[yl], {YL: 1 - yl}, g2sem.at[0])
    norm_second(1)
    norm_second(3)
    norm_first(2)
    arrived(g2.at[1 - yl], g2sem.at[0])
    g3[z] = g2[0] + g2[1]
    for d in zs:
        send(g3.at[z], g3.at[z], {Z: zz(d)}, g3sem.at[d])
    norm_second(2)

    for d in reversed(zs):
        arrived(rd.at[d], rdsem.at[d])
    dsum = ds_[z].astype(F32)
    for d in range(1, NZ):
        dsum = dsum + rd[d].astype(F32)
    dgrad[...] = dsum.astype(BF)

    for d in reversed(zs):
        arrived(g3.at[zz(-d)], g3sem.at[d])
    g4[k] = jnp.sum(g3[...], axis=0)
    for d in (2, 1, 3):
        send(g4.at[k], g4.at[k], {YH: yy(d)}, g4sem.at[d])

    for d in (1, 3, 2):
        arrived(fn.at[yy(d)], fnsem.at[d])
    inv = irms[...]
    inner = jnp.zeros((8, 128), F32)
    for i in range(NZ):
        for q in range(NY):
            b = i * NY + q
            normed = tok[:, b * 128:(b + 1) * 128].astype(F32) * inv
            inner = inner + fn[q, :, i * 128:(i + 1) * 128] * gain[b:b + 1, :] * normed
    inner = jnp.sum(inner, axis=1, keepdims=True) * (1.0 / 4096)
    for i in range(NZ):
        for q in range(NY):
            b = i * NY + q
            cols = slice(b * 128, (b + 1) * 128)
            normed = tok[:, cols].astype(F32) * inv
            scaled = fn[q, :, i * 128:(i + 1) * 128] * gain[b:b + 1, :]
            igrad[:, cols] = (
                gout[:, cols].astype(F32) + inv * (scaled - normed * inner)
            ).astype(BF)

    for d in range(1, NY):
        arrived(g4.at[yy(-d)], g4sem.at[d])
    for i in range(NZ):
        for q in range(NY):
            b = i * NY + q
            ggrad[b:b + 1, :] = g4[q, i:i + 1, :]
    for cp in sends:
        cp.wait_send()


def per_device(
    tokens_in, grad_out, gate_pre, up_pre, gate_weight, up_weight, down_weight, norm_gain
):
    vm = pltpu.VMEM
    dma = pltpu.SemaphoreType.DMA
    scratch = [
        vm((8, 4096), BF),
        vm((8, 4096), BF),
        vm((32, 128), F32),
        vm((3, NZ, 448, 128), BF),
        vm((2, NY, 448, 128), BF),
        vm((2, NY, NX, 2, 2, 8, 1024), BF),
        vm((2, NY, 8, 1024), BF),
        vm((2, NY, 448, 128), F32),
        vm((NY, 448, 128), BF),
        vm((3, 448, 128), BF),
        vm((2, 448, 128), BF),
        vm((2, 224, 128), BF),
        vm((3, 448, 128), F32),
        vm((NY, 448, 128), BF),
        vm((NY, NX, 2, 2, 8, 1024), BF),
        vm((NY, 8, 2, 8, 1024), BF),
        vm((NY, 8, 1024), BF),
        vm((NY, 8, 1024), BF),
        vm((NY, 8, 1024), F32),
        vm((NY, 8, 1024), F32),
        vm((NZ, 448, 128), BF),
        vm((NZ, 448, 128), BF),
        vm((8, 1024), F32),
        vm((8, 8, 128), F32),
        vm((2, 8, 128), F32),
        vm((NZ, 8, 128), F32),
        vm((NY, 8, 128), F32),
        vm((8, 128), F32),
        dma((8,)),
        dma((N_SEND,)),
        dma((3, 2, 4, 2)),
        dma((2, 2, 2, 2)),
        dma((2, 8)),
        dma((2, 4)),
        dma((2, 4)),
        dma((2, 2)),
        dma((2,)),
        dma((2, 2, 2)),
        dma((4, 8)),
        dma((4,)),
        dma((4,)),
        dma((8,)),
        dma((8,)),
        dma((1,)),
        dma((8,)),
        dma((4,)),
    ]
    spec = pl.BlockSpec(memory_space=pltpu.VMEM)
    hbm = pl.BlockSpec(memory_space=pl.ANY)
    igrad, ggrad, dgrad = pl.pallas_call(
        kernel,
        out_shape=(
            jax.ShapeDtypeStruct((8, 4096), BF),
            jax.ShapeDtypeStruct((32, 128), F32),
            jax.ShapeDtypeStruct((448, 128), BF),
        ),
        in_specs=[hbm] * 8,
        out_specs=(spec,) * 3,
        scratch_shapes=scratch,
        compiler_params=pltpu.CompilerParams(
            collective_id=0, has_side_effects=True, vmem_limit_bytes=60 * 1024 * 1024
        ),
    )(
        tokens_in, grad_out, gate_pre.T, up_pre.T, gate_weight.T, up_weight.T, down_weight,
        norm_gain.reshape(32, 128),
    )
    return igrad, ggrad.reshape(4096), dgrad


def solution(mesh):
    finer = Mesh(mesh.devices.reshape(NZ, NY, NX, 2, 2), AXES)
    return jax.shard_map(
        per_device,
        mesh=finer,
        in_specs=(
            P(AXES, None),
            P(AXES, None),
            P(DP, TENSOR),
            P(DP, TENSOR),
            P(DP, TENSOR),
            P(DP, TENSOR),
            P(TENSOR, DP),
            P(),
        ),
        out_specs=(P(AXES, None), P(), P(TENSOR, DP)),
        check_vma=False,
    )
```

time: 97.4 us -> 88.2 us (0.906)
  the two profiles are of different devices: /device:TPU:64 before, /device:TPU:1 now
where the time goes in v3:
time: 88.2 us; the launch traced here: 86.9 us
  Pallas kernels  83.5 us (95%)
  local copies, waits for them, and re-layouts  2.77 us (3%)
    pallas_call x1, Pallas kernels, per_device(): pl.pallas_call(kernel, out_shape=(jax.ShapeDtypeStruct((8, 4096), BF), ja...  83.5 us
    unnamed x7, local copies, waits for them, and re-layouts  2.77 us

profile of v3, /device:TPU:1, one launch (start us, length us, event | category | flops | bytes accessed | tf_op | source)
XLA Modules:
  0.0 86.9 jit_solution(13746236016860105719)
XLA Ops:
  0.6 83.5 %shard_map.103 = (bf16[8,4096]{1,0:T(8,128)(2,1)}, f32[32,128]{1,0:T(8,128)}, bf16[448,128]{1,0:T(8,128)(2,1)}) custom-call(bf16[8,4096]{1,0:T(8,128)(2,1)} %tok_h.1, bf16[8,4096]{1,0:T(8,128)(2,1)} %gout_h.1, bf16[448,128]{1,0:T(8,128)(2,1)} %bitcast.6, bf16[448,128]{1,0:T(8,128)(2,1)} %bitcast.7, bf16[448,128]{1,0:T(8,128)(2,1)} %bitcast.8, ...), custom_call_target="tpu_custom_call" | custom-call | tf_op jit(solution)/shard_map/pallas_call | solution.py:424
  84.2 0.0 copy-start
  84.2 0.0 copy-start.1
  84.2 1.5 %copy.14 = bf16[8,4096]{1,0:T(8,128)(2,1)} copy(bf16[8,4096]{1,0:T(8,128)(2,1)} %get-tuple-element.12) | data formatting | bytes 131072
  85.7 0.0 copy-done.1
  85.7 0.6 copy.15
  86.3 0.0 copy-done
  86.3 0.6 copy.16
Async XLA Ops:
  84.2 2.1 %copy-start = (bf16[448,128]{1,0:T(8,128)(2,1)S(1)}, bf16[448,128]{1,0:T(8,128)(2,1)}, u32[]{:S(2)}) copy-start(bf16[448,128]{1,0:T(8,128)(2,1)} %get-tuple-element.14) | copy-start | bytes 344068
  84.2 1.5 %copy-start.1 = (f32[32,128]{1,0:T(8,128)S(1)}, f32[32,128]{1,0:T(8,128)}, u32[]{:S(2)}) copy-start(f32[32,128]{1,0:T(8,128)} %get-tuple-element.7) | copy-start | bytes 49156

commit v4 on v3

v4 whole, which is shorter than its diff:
```python
import jax
import jax.numpy as jnp
from jax import lax
from jax.experimental import pallas as pl
from jax.experimental.pallas import tpu as pltpu
from jax.sharding import Mesh
from jax.sharding import PartitionSpec as P

AXES = ("dp_0", "dp_1", "tensor_0", "tensor_1", "tensor_2")
Z, YH, X, YL, C = AXES
TENSOR = AXES[2:]
DP = AXES[:2]
BF = jnp.bfloat16
F32 = jnp.float32
MESH = pl.DeviceIdType.MESH
NZ, NY, NX = 8, 4, 4


def dot(a, b, ca, cb):
    return lax.dot_general(a, b, (((ca,), (cb,)), ((), ())), preferred_element_type=F32)


def kernel(
    tok_h, gout_h, gate_h, up_h, gw_h, uw_h, dw_h, gain_h,
    igrad, ggrad, dgrad,
    tok, gout, gain,
    w, gu, a, st, fac, act, sa, ra, rb, part, ga, pn, rc, sx, rx, fs, fn, gn, ds_, rd, gacc,
    g1, g3, g4, irms,
    lsem, ssem, wsem, gsem, s1sem, xsem, csem, rasem, rbsem, gasem, rcsem, rxsem, fnsem, rdsem,
    g1sem, g3sem, g4sem,
):
    z, k, x = lax.axis_index(Z), lax.axis_index(YH), lax.axis_index(X)
    yl, c = lax.axis_index(YL), lax.axis_index(C)
    sends = []

    def send(src, dst, dev, rsem, group):
        if group not in sends:
            sends.append(group)
        pltpu.make_async_remote_copy(
            src_ref=src, dst_ref=dst, send_sem=ssem.at[sends.index(group)], recv_sem=rsem,
            device_id=dev, device_id_type=MESH,
        ).start()

    def arrived(ref, rsem):
        pltpu.make_async_copy(ref, ref, rsem).wait()

    def units(n):
        return a.at[0].reshape(512, 1024).at[pl.ds(0, 8 * n)]

    def zz(d):
        return lax.rem(z + d + NZ, NZ)

    def yy(d):
        return lax.rem(k + d + NY, NY)

    def xx(d):
        return lax.rem(x + d + NX, NX)

    def ee(v, e):
        return lax.rem(v + e, 2)

    ys = [(d, e) for d in (2, 1, 3, 0) for e in (1, 0) if d or e]
    zs = (4, 3, 5, 2, 6, 1, 7)
    ts = [(d, e, f) for d in (2, 1, 3, 0) for e in (1, 0) for f in (1, 0) if d or e or f]

    def ts_dev(d, e, f):
        return {X: xx(d), YL: ee(yl, e), C: ee(c, f)}

    def t_of(xs, ls, cs):
        return xs * 4 + ls * 2 + cs

    def ys_dev(d, e):
        return {YH: yy(d), YL: ee(yl, e)}

    peers = [{Z: zz(d)} for d in zs]
    peers += [ys_dev(d, e) for d, e in ys] + [ts_dev(*v) for v in ts if v != (0, 1, 0)]
    barrier = pltpu.get_barrier_semaphore()
    for p in peers:
        pl.semaphore_signal(barrier, inc=1, device_id=p, device_id_type=MESH)

    loads = [
        (gout_h, gout), (tok_h, tok), (dw_h, w.at[0, z]), (gate_h, gu.at[0, k]),
        (up_h, gu.at[1, k]), (gw_h, w.at[1, z]), (uw_h, w.at[2, z]), (gain_h, gain),
    ]
    loads = [pltpu.make_async_copy(s, d, lsem.at[i]) for i, (s, d) in enumerate(loads)]
    for cp in loads:
        cp.start()

    loads[0].wait()
    for q in range(NY):
        for i in range(NZ):
            col = (i * NY + q) * 128
            st[0, q, :, i * 128:(i + 1) * 128] = gout[:, col:col + 128]
    a[0, k, x, yl, c] = st[0, k]
    loads[1].wait()
    tf = tok[...].astype(F32)
    inv = lax.rsqrt(jnp.mean(tf * tf, axis=1, keepdims=True) + 1e-05)
    irms[...] = jnp.broadcast_to(inv, (8, 128))
    for q in range(NY):
        for i in range(NZ):
            col = (i * NY + q) * 128
            st[1, q, :, i * 128:(i + 1) * 128] = (tf[:, col:col + 128] * inv).astype(BF)
    a[1, k, x, yl, c] = st[1, k]
    for cp in loads[2:]:
        cp.wait()
    pl.semaphore_wait(barrier, len(peers))

    def half(ref, h):
        return ref.at[pl.ds(224 * h, 224)]

    class Ring:
        def __init__(self, buf, at, me, n, left, right, sem, group):
            self.buf, self.at, self.me, self.n, self.sem, self.group = buf, at, me, n, sem, group
            self.devs = (right, left)

        def put(self, slot, way, step, h):
            p = half(self.buf.at[slot], h)
            send(p, p, self.devs[way], self.sem.at[way, step, h], self.group)

        def first(self):
            for i in range(2):
                for way in range(2):
                    self.put(self.me, way, 0, i ^ way)

        def got(self, s, way, h):
            slot = self.at(-s if way == 0 else s)
            arrived(half(self.buf.at[slot], h), self.sem.at[way, s - 1, h])
            return slot

        def nxt(self, s, parts=(0, 1)):
            for i in parts:
                for way in range(2):
                    slot = self.got(s, way, i ^ way)
                    if s + 1 < self.n // 2 or i == 0:
                        self.put(slot, way, s, i ^ way)

        def last(self):
            for way in range(2):
                self.got(self.n // 2, way, way)

    zl, zr, kl, kr = {Z: zz(-1)}, {Z: zz(1)}, {YH: yy(-1)}, {YH: yy(1)}
    dwr, gwr, uwr = [Ring(w.at[i], zz, z, NZ, zl, zr, wsem.at[i], "w%d" % i) for i in range(3)]
    gater, upr = [Ring(gu.at[i], yy, k, NY, kl, kr, gsem.at[i], "gu") for i in range(2)]
    gar = Ring(ga, yy, k, NY, kl, kr, gasem, "ga")
    core = {C: 1 - c}

    def s1_send(i):
        for d, e in ys:
            send(st.at[i, yy(d)], a.at[i, k, x, yl, c], ys_dev(d, e), s1sem.at[i], "s1")

    def s1_wait(i):
        arrived(units(7), s1sem.at[i])

    def unit(i, xs, cs):
        return a.at[i, :, xs, :, cs]

    def x_send(i):
        for d in (2, 1, 3):
            send(unit(i, x, c), unit(i, x, c), {X: xx(d)}, xsem.at[i, d], "x%d" % i)
        send(unit(i, x, c), unit(i, x, c), core, csem.at[i], "x%d" % i)

    def x_wait(i):
        for d in (1, 3, 2):
            u = unit(i, xx(-d), c)
            arrived(u, xsem.at[i, d])
            send(u, u, core, csem.at[i], "x%d" % i)

    def core_wait(i):
        arrived(units(32), csem.at[i])

    dwr.first()
    s1_send(0)
    s1_send(1)
    gater.first()
    upr.first()
    dwr.nxt(1)
    s1_wait(0)
    x_send(0)
    dwr.nxt(2)
    s1_wait(1)
    x_send(1)
    dwr.nxt(3)
    gwr.first()
    uwr.first()
    x_wait(0)
    dwr.last()
    core_wait(0)

    down = jnp.concatenate([w[0, i] for i in range(NZ)], axis=1)

    def partial(d, e):
        rows = [a.at[0, yy(v)].reshape(128, 1024)[...] for v in (d, e)]
        both = dot(down, jnp.concatenate(rows, axis=0), 1, 1)
        return both[:, :128], both[:, 128:]

    def own_half(n, dev, h):
        rows = slice(224 * h, 224 * h + 224)
        sa[2 * n, rows] = part[n, rows].astype(BF)
        send(half(sa.at[2 * n], h), half(ra.at[n], h), dev, rasem.at[n], "ga")

    far, part[0] = partial(2, 1)
    sa[1] = far.astype(BF)
    send(half(sa.at[1], 0), rb.at[0], kr, rbsem.at[0], "ga")
    send(half(sa.at[1], 1), rb.at[1], kl, rbsem.at[1], "ga")
    own_half(0, kr, 1)
    part[1], part[2] = partial(3, 0)
    own_half(1, kl, 0)

    gwr.nxt(1)
    uwr.nxt(1)
    x_wait(1)

    for n, (dev, h) in enumerate(((kr, 0), (kl, 1))):
        rows = slice(224 * h, 224 * h + 224)
        arrived(rb.at[n], rbsem.at[n])
        sa[2 * n, rows] = (part[n, rows] + rb[n].astype(F32)).astype(BF)
        send(half(sa.at[2 * n], h), half(ra.at[n], h), dev, rasem.at[n], "ga")
    gater.nxt(1)
    gwr.nxt(2)
    upr.nxt(1)
    core_wait(1)
    uwr.nxt(2)
    gwr.nxt(3)
    uwr.nxt(3)
    for n in range(2):
        arrived(ra.at[n], rasem.at[n])
    ga[k] = (part[2] + ra[0].astype(F32) + ra[1].astype(F32)).astype(BF)
    gar.first()

    gater.last()
    upr.last()
    for j in range(NY):
        gv = gu[0, j].astype(F32)
        uv = gu[1, j].astype(F32)
        sg = jax.nn.sigmoid(gv)
        sv = gv * sg
        fac[0, j] = uv * sg * (1.0 + gv * (1.0 - sg))
        fac[1, j] = sv
        act[j] = (sv * uv).astype(BF)

    acts = jnp.concatenate([act[j] for j in range(NY)], axis=1)
    rows_all = a.at[0].reshape(512, 1024)
    for i in range(NZ // 2):
        pair = dot(acts, rows_all[:, i * 256:(i + 1) * 256], 1, 0)
        ds_[2 * i] = pair[:, :128].astype(BF)
        ds_[2 * i + 1] = pair[:, 128:].astype(BF)

    def down_put(way, slot, step, h):
        send(
            half(ds_.at[slot], h), half(rd.at[way, step], h), (zr, zl)[way],
            rdsem.at[way, step, h], "down",
        )

    def down_add(way, slot, step, h):
        arrived(half(rd.at[way, step], h), rdsem.at[way, step, h])
        rows = slice(224 * h, 224 * h + 224)
        ds_[slot, rows] = (
            ds_[slot, rows].astype(F32) + rd[way, step, rows].astype(F32)
        ).astype(BF)

    def down_next(s):
        for i in range(2 if s > 1 else 1):
            for way in range(2):
                slot = zz(4 - s if way == 0 else s - 4)
                down_add(way, slot, s - 1, i ^ way)
                down_put(way, slot, s, i ^ way)

    for way in range(2):
        down_put(way, zz(4), 0, way)
    for way in range(2):
        down_put(way, zz(3 if way == 0 else -3), 1, 1 - way)

    gwr.last()
    uwr.last()

    def norm_part(d):
        j = yy(-d)
        gj = ga[j].astype(F32)
        both = jnp.concatenate([(gj * fac[0, j]).astype(BF), (gj * fac[1, j]).astype(BF)], axis=0)
        for i in range(NZ // 2):
            cols = jnp.concatenate(
                [
                    jnp.concatenate([w[1, 2 * i], w[2, 2 * i]], axis=0),
                    jnp.concatenate([w[1, 2 * i + 1], w[2, 2 * i + 1]], axis=0),
                ],
                axis=1,
            )
            block = dot(both, cols, 0, 0)
            lanes = slice(i * 256, (i + 1) * 256)
            for q in range(16):
                pn[d, q // 4, (q // 2) % 2, q % 2, :, lanes] = block[q * 8:(q + 1) * 8].astype(BF)
        send(pn.at[d, :, :, 1 - c], rc.at[d], core, rcsem.at[d], "norm")

    def norm_core(d):
        arrived(rc.at[d], rcsem.at[d])
        for i in range(NX):
            for j in range(2):
                sx[d, i, j] = (pn[d, i, j, c].astype(F32) + rc[d, i, j].astype(F32)).astype(BF)
        for e in (2, 1, 3):
            send(sx.at[d, xx(e)], rx.at[d, e], {X: xx(e)}, rxsem.at[d], "norm")

    def norm_x(d):
        arrived(units(6), rxsem.at[d])
        for f in (1, 0):
            v = ee(yl, f)
            rows = sx[d, x, v].astype(F32)
            for e in range(1, NX):
                rows = rows + rx[d, e, v].astype(F32)
            if d or f:
                fs[d, f] = rows.astype(BF)
                send(fs.at[d, f], fn.at[k, yl], ys_dev(-d, f), fnsem.at[0], "norm")
            else:
                fn[k, yl] = rows.astype(BF)

    def gain_part(d):
        add = gacc[...]
        for q in range(16):
            at = (q // 4, (q // 2) % 2, q % 2)
            add = add + pn[(d,) + at].astype(F32) * a[(1, yy(-d)) + at].astype(F32)
        gacc[...] = add

    gacc[...] = jnp.zeros((8, 1024), F32)
    norm_part(0)
    gar.nxt(1, (0,))
    norm_core(0)
    gar.nxt(1, (1,))
    norm_part(1)
    norm_part(3)
    down_next(1)
    norm_core(1)
    norm_core(3)
    for d in (0, 1, 3):
        gain_part(d)
    gar.last()
    norm_part(2)

    gain_part(2)
    mine = t_of(x, yl, c)
    for i in range(NZ):
        g1[mine, i:i + 1, :] = jnp.sum(gacc[:, i * 128:(i + 1) * 128], axis=0, keepdims=True)
    for d, e, f in ts:
        send(g1.at[mine], g1.at[mine], ts_dev(d, e, f), g1sem.at[0], "g1")

    norm_core(2)
    down_next(2)
    for d in (0, 1, 3):
        norm_x(d)
    arrived(g1.at[pl.ds(0, 15)], g1sem.at[0])
    g3[z] = jnp.sum(g1[...], axis=0)
    for d in zs:
        send(g3.at[z], g3.at[z], {Z: zz(d)}, g3sem.at[0], "g3")
    norm_x(2)
    down_next(3)

    arrived(g3.at[pl.ds(0, 7)], g3sem.at[0])
    g4[k] = jnp.sum(g3[...], axis=0)
    for d in (2, 1, 3):
        send(g4.at[k], g4.at[k], {YH: yy(d)}, g4sem.at[0], "g3")

    for h in range(2):
        for way in range(2):
            down_add(way, z, 3, h)
    outs = [pltpu.make_async_copy(ds_.at[z], dgrad, lsem.at[0])]
    outs[0].start()

    arrived(units(7), fnsem.at[0])
    for q in range(NY):
        gn[q] = fn[q, 0].astype(F32) + fn[q, 1].astype(F32)
    inv = irms[...]
    inner = jnp.zeros((8, 128), F32)
    for i in range(NZ):
        for q in range(NY):
            b = i * NY + q
            normed = tok[:, b * 128:(b + 1) * 128].astype(F32) * inv
            inner = inner + gn[q, :, i * 128:(i + 1) * 128] * gain[b:b + 1, :] * normed
    inner = jnp.sum(inner, axis=1, keepdims=True) * (1.0 / 4096)
    for i in range(NZ):
        for q in range(NY):
            b = i * NY + q
            cols = slice(b * 128, (b + 1) * 128)
            normed = tok[:, cols].astype(F32) * inv
            scaled = gn[q, :, i * 128:(i + 1) * 128] * gain[b:b + 1, :]
            tok[:, cols] = (
                gout[:, cols].astype(F32) + inv * (scaled - normed * inner)
            ).astype(BF)

    outs.append(pltpu.make_async_copy(tok, igrad, lsem.at[1]))
    outs[1].start()
    arrived(g4.at[pl.ds(0, 3)], g4sem.at[0])
    for i in range(NZ):
        for q in range(NY):
            b = i * NY + q
            gain[b:b + 1, :] = g4[q, i:i + 1, :]
    outs.append(pltpu.make_async_copy(gain, ggrad, lsem.at[2]))
    outs[2].start()
    sent = {
        "w0": w.at[0, pl.ds(0, 7)], "w1": w.at[0, pl.ds(0, 7)], "w2": w.at[0, pl.ds(0, 7)],
        "gu": w.at[0, pl.ds(0, 6)], "ga": w.at[0, pl.ds(0, 6)], "down": w.at[0, pl.ds(0, 7)],
        "s1": units(14), "x0": units(56), "x1": units(56), "norm": units(63),
        "g1": g1.at[pl.ds(0, 15)], "g3": g1.at[pl.ds(0, 10)],
    }
    for i, group in enumerate(sends):
        arrived(sent[group], ssem.at[i])
    for cp in outs:
        cp.wait()


def per_device(
    tokens_in, grad_out, gate_pre, up_pre, gate_weight, up_weight, down_weight, norm_gain
):
    vm = pltpu.VMEM
    dma = pltpu.SemaphoreType.DMA
    scratch = [
        vm((8, 4096), BF),
        vm((8, 4096), BF),
        vm((32, 128), F32),
        vm((3, NZ, 448, 128), BF),
        vm((2, NY, 448, 128), BF),
        vm((2, NY, NX, 2, 2, 8, 1024), BF),
        vm((2, NY, 8, 1024), BF),
        vm((2, NY, 448, 128), F32),
        vm((NY, 448, 128), BF),
        vm((3, 448, 128), BF),
        vm((2, 448, 128), BF),
        vm((2, 224, 128), BF),
        vm((3, 448, 128), F32),
        vm((NY, 448, 128), BF),
        vm((NY, NX, 2, 2, 8, 1024), BF),
        vm((NY, NX, 2, 8, 1024), BF),
        vm((NY, NX, 2, 8, 1024), BF),
        vm((NY, NX, 2, 8, 1024), BF),
        vm((NY, 2, 8, 1024), BF),
        vm((NY, 2, 8, 1024), BF),
        vm((NY, 8, 1024), F32),
        vm((NZ, 448, 128), BF),
        vm((2, 4, 448, 128), BF),
        vm((8, 1024), F32),
        vm((16, 8, 128), F32),
        vm((NZ, 8, 128), F32),
        vm((NY, 8, 128), F32),
        vm((8, 128), F32),
        dma((8,)),
        dma((12,)),
        dma((3, 2, 4, 2)),
        dma((2, 2, 2, 2)),
        dma((2,)),
        dma((2, 4)),
        dma((2,)),
        dma((2,)),
        dma((2,)),
        dma((2, 2, 2)),
        dma((4,)),
        dma((4,)),
        dma((1,)),
        dma((2, 4, 2)),
        dma((1,)),
        dma((1,)),
        dma((1,)),
    ]
    hbm = pl.BlockSpec(memory_space=pl.ANY)
    igrad, ggrad, dgrad = pl.pallas_call(
        kernel,
        out_shape=(
            jax.ShapeDtypeStruct((8, 4096), BF),
            jax.ShapeDtypeStruct((32, 128), F32),
            jax.ShapeDtypeStruct((448, 128), BF),
        ),
        in_specs=[hbm] * 8,
        out_specs=(hbm,) * 3,
        scratch_shapes=scratch,
        compiler_params=pltpu.CompilerParams(
            collective_id=0, has_side_effects=True, vmem_limit_bytes=60 * 1024 * 1024
        ),
    )(
        tokens_in, grad_out, gate_pre.T, up_pre.T, gate_weight.T, up_weight.T, down_weight,
        norm_gain.reshape(32, 128),
    )
    return igrad, ggrad.reshape(4096), dgrad


def solution(mesh):
    finer = Mesh(mesh.devices.reshape(NZ, NY, NX, 2, 2), AXES)
    return jax.shard_map(
        per_device,
        mesh=finer,
        in_specs=(
            P(AXES, None),
            P(AXES, None),
            P(DP, TENSOR),
            P(DP, TENSOR),
            P(DP, TENSOR),
            P(DP, TENSOR),
            P(TENSOR, DP),
            P(),
        ),
        out_specs=(P(AXES, None), P(), P(TENSOR, DP)),
        check_vma=False,
    )
```

time: 88.2 us -> 75.6 us (0.86); the launches traced: 86.9 us -> 75.4 us
  Pallas kernels: 83.5 us -> 72 us
    pallas_call x1, Pallas kernels: 83.5 us -> 72 us  [per_device(): pl.pallas_call(kernel, out_shape=(jax.ShapeDtypeStruct((8, 4096), BF), ja...]
where the time goes in v4:
time: 75.6 us; the launch traced here: 75.4 us
  Pallas kernels  72 us (95%)
  local copies, waits for them, and re-layouts  2.77 us (4%)
    pallas_call x1, Pallas kernels, per_device(): pl.pallas_call(kernel, out_shape=(jax.ShapeDtypeStruct((8, 4096), BF), ja...  72 us
    unnamed x7, local copies, waits for them, and re-layouts  2.77 us

profile of v4, /device:TPU:1, one launch (start us, length us, event | category | flops | bytes accessed | tf_op | source)
XLA Modules:
  0.0 75.4 jit_solution(1427716069801330461)
XLA Ops:
  0.6 72.0 %shard_map.103 = (bf16[8,4096]{1,0:T(8,128)(2,1)}, f32[32,128]{1,0:T(8,128)}, bf16[448,128]{1,0:T(8,128)(2,1)}) custom-call(bf16[8,4096]{1,0:T(8,128)(2,1)} %tok_h.1, bf16[8,4096]{1,0:T(8,128)(2,1)} %gout_h.1, bf16[448,128]{1,0:T(8,128)(2,1)} %bitcast.6, bf16[448,128]{1,0:T(8,128)(2,1)} %bitcast.7, bf16[448,128]{1,0:T(8,128)(2,1)} %bitcast.8, ...), custom_call_target="tpu_custom_call" | custom-call | tf_op jit(solution)/shard_map/pallas_call | solution.py:461
  72.6 0.0 copy-start
  72.6 0.0 copy-start.1
  72.6 1.5 %copy.14 = bf16[8,4096]{1,0:T(8,128)(2,1)} copy(bf16[8,4096]{1,0:T(8,128)(2,1)} %get-tuple-element.12) | data formatting | bytes 131072
  74.1 0.0 copy-done.1
  74.1 0.6 copy.15
  74.7 0.0 copy-done
  74.7 0.6 copy.16
Async XLA Ops:
  72.6 2.1 %copy-start = (bf16[448,128]{1,0:T(8,128)(2,1)S(1)}, bf16[448,128]{1,0:T(8,128)(2,1)}, u32[]{:S(2)}) copy-start(bf16[448,128]{1,0:T(8,128)(2,1)} %get-tuple-element.14) | copy-start | bytes 344068
  72.6 1.5 %copy-start.1 = (f32[32,128]{1,0:T(8,128)S(1)}, f32[32,128]{1,0:T(8,128)}, u32[]{:S(2)}) copy-start(f32[32,128]{1,0:T(8,128)} %get-tuple-element.7) | copy-start | bytes 49156

commit v5 on v4

--- a/solution.py
+++ b/solution.py
@@ -74,24 +74,96 @@
 
     peers = [{Z: zz(d)} for d in zs]
     peers += [ys_dev(d, e) for d, e in ys] + [ts_dev(*v) for v in ts if v != (0, 1, 0)]
-    barrier = pltpu.get_barrier_semaphore()
-    for p in peers:
-        pl.semaphore_signal(barrier, inc=1, device_id=p, device_id_type=MESH)
-
     loads = [
         (gout_h, gout), (tok_h, tok), (dw_h, w.at[0, z]), (gate_h, gu.at[0, k]),
         (up_h, gu.at[1, k]), (gw_h, w.at[1, z]), (uw_h, w.at[2, z]), (gain_h, gain),
     ]
     loads = [pltpu.make_async_copy(s, d, lsem.at[i]) for i, (s, d) in enumerate(loads)]
-    for cp in loads:
-        cp.start()
+    for i in (0, 2, 3, 4, 1, 5, 6, 7):
+        loads[i].start()
+    barrier = pltpu.get_barrier_semaphore()
+    for p in peers:
+        pl.semaphore_signal(barrier, inc=1, device_id=p, device_id_type=MESH)
 
     loads[0].wait()
     for q in range(NY):
         for i in range(NZ):
             col = (i * NY + q) * 128
             st[0, q, :, i * 128:(i + 1) * 128] = gout[:, col:col + 128]
+    loads[2].wait()
+    pl.semaphore_wait(barrier, len(peers))
+
+    def half(ref, h):
+        return ref.at[pl.ds(224 * h, 224)]
+
+    class Ring:
+        def __init__(self, buf, at, me, n, left, right, sem, group):
+            self.buf, self.at, self.me, self.n, self.sem, self.group = buf, at, me, n, sem, group
+            self.devs = (right, left)
+
+        def put(self, slot, way, step, h):
+            p = half(self.buf.at[slot], h)
+            send(p, p, self.devs[way], self.sem.at[way, step, h], self.group)
+
+        def first(self):
+            for i in range(2):
+                for way in range(2):
+                    self.put(self.me, way, 0, i ^ way)
+
+        def got(self, s, way, h):
+            slot = self.at(-s if way == 0 else s)
+            arrived(half(self.buf.at[slot], h), self.sem.at[way, s - 1, h])
+            return slot
+
+        def nxt(self, s, parts=(0, 1)):
+            for i in parts:
+                for way in range(2):
+                    slot = self.got(s, way, i ^ way)
+                    if s + 1 < self.n // 2 or i == 0:
+                        self.put(slot, way, s, i ^ way)
+
+        def last(self):
+            for way in range(2):
+                self.got(self.n // 2, way, way)
+
+    zl, zr, kl, kr = {Z: zz(-1)}, {Z: zz(1)}, {YH: yy(-1)}, {YH: yy(1)}
+    dwr, gwr, uwr = [Ring(w.at[i], zz, z, NZ, zl, zr, wsem.at[i], "w%d" % i) for i in range(3)]
+    gater, upr = [Ring(gu.at[i], yy, k, NY, kl, kr, gsem.at[i], "gu") for i in range(2)]
+    gar = Ring(ga, yy, k, NY, kl, kr, gasem, "ga")
+    core = {C: 1 - c}
+
+    def s1_send(i):
+        for d, e in ys:
+            send(st.at[i, yy(d)], a.at[i, k, x, yl, c], ys_dev(d, e), s1sem.at[i], "s1")
+
+    def s1_wait(i):
+        arrived(units(7), s1sem.at[i])
+
+    def unit(i, xs, cs):
+        return a.at[i, :, xs, :, cs]
+
+    def x_send(i):
+        for d in (2, 1, 3):
+            send(unit(i, x, c), unit(i, x, c), {X: xx(d)}, xsem.at[i, d], "x%d" % i)
+        send(unit(i, x, c), unit(i, x, c), core, csem.at[i], "x%d" % i)
+
+    def x_wait(i):
+        for d in (1, 3, 2):
+            u = unit(i, xx(-d), c)
+            arrived(u, xsem.at[i, d])
+            send(u, u, core, csem.at[i], "x%d" % i)
+
+    def core_wait(i):
+        arrived(units(32), csem.at[i])
+
+    dwr.first()
+    s1_send(0)
+    for cp in loads[3:5]:
+        cp.wait()
+    gater.first()
+    upr.first()
     a[0, k, x, yl, c] = st[0, k]
+
     loads[1].wait()
     tf = tok[...].astype(F32)
     inv = lax.rsqrt(jnp.mean(tf * tf, axis=1, keepdims=True) + 1e-05)
@@ -101,89 +173,20 @@
             col = (i * NY + q) * 128
             st[1, q, :, i * 128:(i + 1) * 128] = (tf[:, col:col + 128] * inv).astype(BF)
     a[1, k, x, yl, c] = st[1, k]
-    for cp in loads[2:]:
+    s1_send(1)
+    for cp in loads[5:]:
         cp.wait()
-    pl.semaphore_wait(barrier, len(peers))
-
-    def half(ref, h):
-        return ref.at[pl.ds(224 * h, 224)]
-
-    class Ring:
-        def __init__(self, buf, at, me, n, left, right, sem, group):
-            self.buf, self.at, self.me, self.n, self.sem, self.group = buf, at, me, n, sem, group
-            self.devs = (right, left)
-
-        def put(self, slot, way, step, h):
-            p = half(self.buf.at[slot], h)
-            send(p, p, self.devs[way], self.sem.at[way, step, h], self.group)
-
-        def first(self):
-            for i in range(2):
-                for way in range(2):
-                    self.put(self.me, way, 0, i ^ way)
-
-        def got(self, s, way, h):
-            slot = self.at(-s if way == 0 else s)
-            arrived(half(self.buf.at[slot], h), self.sem.at[way, s - 1, h])
-            return slot
-
-        def nxt(self, s, parts=(0, 1)):
-            for i in parts:
-                for way in range(2):
-                    slot = self.got(s, way, i ^ way)
-                    if s + 1 < self.n // 2 or i == 0:
-                        self.put(slot, way, s, i ^ way)
-
-        def last(self):
-            for way in range(2):
-                self.got(self.n // 2, way, way)
-
-    zl, zr, kl, kr = {Z: zz(-1)}, {Z: zz(1)}, {YH: yy(-1)}, {YH: yy(1)}
-    dwr, gwr, uwr = [Ring(w.at[i], zz, z, NZ, zl, zr, wsem.at[i], "w%d" % i) for i in range(3)]
-    gater, upr = [Ring(gu.at[i], yy, k, NY, kl, kr, gsem.at[i], "gu") for i in range(2)]
-    gar = Ring(ga, yy, k, NY, kl, kr, gasem, "ga")
-    core = {C: 1 - c}
-
-    def s1_send(i):
-        for d, e in ys:
-            send(st.at[i, yy(d)], a.at[i, k, x, yl, c], ys_dev(d, e), s1sem.at[i], "s1")
-
-    def s1_wait(i):
-        arrived(units(7), s1sem.at[i])
-
-    def unit(i, xs, cs):
-        return a.at[i, :, xs, :, cs]
-
-    def x_send(i):
-        for d in (2, 1, 3):
-            send(unit(i, x, c), unit(i, x, c), {X: xx(d)}, xsem.at[i, d], "x%d" % i)
-        send(unit(i, x, c), unit(i, x, c), core, csem.at[i], "x%d" % i)
-
-    def x_wait(i):
-        for d in (1, 3, 2):
-            u = unit(i, xx(-d), c)
-            arrived(u, xsem.at[i, d])
-            send(u, u, core, csem.at[i], "x%d" % i)
-
-    def core_wait(i):
-        arrived(units(32), csem.at[i])
-
-    dwr.first()
-    s1_send(0)
-    s1_send(1)
-    gater.first()
-    upr.first()
+
     dwr.nxt(1)
     s1_wait(0)
     x_send(0)
     dwr.nxt(2)
-    s1_wait(1)
-    x_send(1)
     dwr.nxt(3)
     gwr.first()
     uwr.first()
     x_wait(0)
     dwr.last()
+    gater.nxt(1)
     core_wait(0)
 
     down = jnp.concatenate([w[0, i] for i in range(NZ)], axis=1)
@@ -208,20 +211,19 @@
 
     gwr.nxt(1)
     uwr.nxt(1)
-    x_wait(1)
+    s1_wait(1)
+    x_send(1)
 
     for n, (dev, h) in enumerate(((kr, 0), (kl, 1))):
         rows = slice(224 * h, 224 * h + 224)
         arrived(rb.at[n], rbsem.at[n])
         sa[2 * n, rows] = (part[n, rows] + rb[n].astype(F32)).astype(BF)
         send(half(sa.at[2 * n], h), half(ra.at[n], h), dev, rasem.at[n], "ga")
-    gater.nxt(1)
+    upr.nxt(1)
     gwr.nxt(2)
-    upr.nxt(1)
-    core_wait(1)
     uwr.nxt(2)
+    x_wait(1)
     gwr.nxt(3)
-    uwr.nxt(3)
     for n in range(2):
         arrived(ra.at[n], rasem.at[n])
     ga[k] = (part[2] + ra[0].astype(F32) + ra[1].astype(F32)).astype(BF)
@@ -237,6 +239,7 @@
         fac[0, j] = uv * sg * (1.0 + gv * (1.0 - sg))
         fac[1, j] = sv
         act[j] = (sv * uv).astype(BF)
+    uwr.nxt(3)
 
     acts = jnp.concatenate([act[j] for j in range(NY)], axis=1)
     rows_all = a.at[0].reshape(512, 1024)
@@ -269,9 +272,6 @@
         down_put(way, zz(4), 0, way)
     for way in range(2):
         down_put(way, zz(3 if way == 0 else -3), 1, 1 - way)
-
-    gwr.last()
-    uwr.last()
 
     def norm_part(d):
         j = yy(-d)
@@ -320,15 +320,16 @@
         gacc[...] = add
 
     gacc[...] = jnp.zeros((8, 1024), F32)
+    gar.nxt(1, (0,))
+    gwr.last()
+    uwr.last()
     norm_part(0)
-    gar.nxt(1, (0,))
-    norm_core(0)
     gar.nxt(1, (1,))
     norm_part(1)
     norm_part(3)
+    norm_core(0)
     down_next(1)
-    norm_core(1)
-    norm_core(3)
+    core_wait(1)
     for d in (0, 1, 3):
         gain_part(d)
     gar.last()
@@ -341,21 +342,28 @@
     for d, e, f in ts:
         send(g1.at[mine], g1.at[mine], ts_dev(d, e, f), g1sem.at[0], "g1")
 
-    norm_core(2)
+    for d in (1, 3, 2):
+        norm_core(d)
+    norm_x(0)
     down_next(2)
-    for d in (0, 1, 3):
+    arrived(g1.at[pl.ds(0, 15)], g1sem.at[0])
+
+    @pl.when(c == 1)
+    def _():
+        g3[z] = jnp.sum(g1[...], axis=0)
+        for d in zs:
+            send(g3.at[z], g3.at[z], {Z: zz(d)}, g3sem.at[0], "g3")
+
+    for d in (1, 3, 2):
         norm_x(d)
-    arrived(g1.at[pl.ds(0, 15)], g1sem.at[0])
-    g3[z] = jnp.sum(g1[...], axis=0)
-    for d in zs:
-        send(g3.at[z], g3.at[z], {Z: zz(d)}, g3sem.at[0], "g3")
-    norm_x(2)
     down_next(3)
 
-    arrived(g3.at[pl.ds(0, 7)], g3sem.at[0])
-    g4[k] = jnp.sum(g3[...], axis=0)
-    for d in (2, 1, 3):
-        send(g4.at[k], g4.at[k], {YH: yy(d)}, g4sem.at[0], "g3")
+    @pl.when(c == 1)
+    def _():
+        arrived(g3.at[pl.ds(0, 7)], g3sem.at[0])
+        g4[k] = jnp.sum(g3[...], axis=0)
+        for d in (2, 1, 3):
+            send(g4.at[k], g4.at[k], {YH: yy(d)}, g4sem.at[0], "g3")
 
     for h in range(2):
         for way in range(2):
@@ -386,7 +394,16 @@
 
     outs.append(pltpu.make_async_copy(tok, igrad, lsem.at[1]))
     outs[1].start()
-    arrived(g4.at[pl.ds(0, 3)], g4sem.at[0])
+
+    @pl.when(c == 1)
+    def _():
+        arrived(g4.at[pl.ds(0, 3)], g4sem.at[0])
+        send(g4, g4, core, g4sem.at[1], "g4")
+
+    @pl.when(c == 0)
+    def _():
+        arrived(g4, g4sem.at[1])
+
     for i in range(NZ):
         for q in range(NY):
             b = i * NY + q
@@ -397,10 +414,32 @@
         "w0": w.at[0, pl.ds(0, 7)], "w1": w.at[0, pl.ds(0, 7)], "w2": w.at[0, pl.ds(0, 7)],
         "gu": w.at[0, pl.ds(0, 6)], "ga": w.at[0, pl.ds(0, 6)], "down": w.at[0, pl.ds(0, 7)],
         "s1": units(14), "x0": units(56), "x1": units(56), "norm": units(63),
-        "g1": g1.at[pl.ds(0, 15)], "g3": g1.at[pl.ds(0, 10)],
+        "g1": g1.at[pl.ds(0, 15)], "g3": g1.at[pl.ds(0, 10)], "g4": g4,
     }
-    for i, group in enumerate(sends):
-        arrived(sent[group], ssem.at[i])
+
+    def all_sent(late):
+        for i, group in enumerate(sends):
+            if (group in ("g3", "g4")) == late:
+                arrived(sent[group], ssem.at[i])
+
+    all_sent(False)
+
+    @pl.when(c == 1)
+    def _():
+        all_sent(True)
+
+    for cp in outs:
+        cp.wait()
+
+
+def hand_on(i0, i1, i2, o0, o1, o2, b0, b1, b2, sem):
+    ins = [pltpu.make_async_copy(s, d, sem.at[0, n]) for n, (s, d) in enumerate(((i0, b0), (i1, b1), (i2, b2)))]
+    outs = [pltpu.make_async_copy(s, d, sem.at[1, n]) for n, (s, d) in enumerate(((b0, o0), (b1, o1), (b2, o2)))]
+    for cp in ins:
+        cp.start()
+    for i, o in zip(ins, outs):
+        i.wait()
+        o.start()
     for cp in outs:
         cp.wait()
 
@@ -440,7 +479,7 @@
         vm((NY, 8, 128), F32),
         vm((8, 128), F32),
         dma((8,)),
-        dma((12,)),
+        dma((13,)),
         dma((3, 2, 4, 2)),
         dma((2, 2, 2, 2)),
         dma((2,)),
@@ -455,16 +494,17 @@
         dma((2, 4, 2)),
         dma((1,)),
         dma((1,)),
-        dma((1,)),
+        dma((2,)),
     ]
     hbm = pl.BlockSpec(memory_space=pl.ANY)
-    igrad, ggrad, dgrad = pl.pallas_call(
+    shapes = (
+        jax.ShapeDtypeStruct((8, 4096), BF),
+        jax.ShapeDtypeStruct((32, 128), F32),
+        jax.ShapeDtypeStruct((448, 128), BF),
+    )
+    results = pl.pallas_call(
         kernel,
-        out_shape=(
-            jax.ShapeDtypeStruct((8, 4096), BF),
-            jax.ShapeDtypeStruct((32, 128), F32),
-            jax.ShapeDtypeStruct((448, 128), BF),
-        ),
+        out_shape=shapes,
         in_specs=[hbm] * 8,
         out_specs=(hbm,) * 3,
         scratch_shapes=scratch,
@@ -475,6 +515,14 @@
         tokens_in, grad_out, gate_pre.T, up_pre.T, gate_weight.T, up_weight.T, down_weight,
         norm_gain.reshape(32, 128),
     )
+    igrad, ggrad, dgrad = pl.pallas_call(
+        hand_on,
+        out_shape=shapes,
+        in_specs=[hbm] * 3,
+        out_specs=(hbm,) * 3,
+        scratch_shapes=[vm(v.shape, v.dtype) for v in shapes] + [dma((2, 3))],
+        compiler_params=pltpu.CompilerParams(vmem_limit_bytes=60 * 1024 * 1024),
+    )(*results)
     return igrad, ggrad.reshape(4096), dgrad
 
 

time: 75.6 us -> 72.3 us (0.956)
  local copies, waits for them, and re-layouts: 2.77 us -> 0 us
    unnamed x7 -> x0, local copies, waits for them, and re-layouts: 2.77 us -> none
    pallas_call x1 -> x2, Pallas kernels: 72 us -> 71.5 us  [the longest x1 69.9 us: per_device(): pl.pallas_call(kernel, out_shape=shapes, in_specs=[hbm] * 8, out_specs=(h...]
where the time goes in v5:
time: 72.3 us; the launch traced here: 72.2 us
  Pallas kernels  71.5 us (99%)
    pallas_call x1, Pallas kernels, per_device(): pl.pallas_call(kernel, out_shape=shapes, in_specs=[hbm] * 8, out_specs=(h...  69.9 us
    pallas_call x1, Pallas kernels, per_device(): pl.pallas_call(hand_on, out_shape=shapes, in_specs=[hbm] * 3, out_specs=(...  1.65 us

profile of v5, /device:TPU:1, one launch (start us, length us, event | category | flops | bytes accessed | tf_op | source)
XLA Modules:
  0.0 72.2 jit_solution(11867544798540921954)
XLA Ops:
  0.6 69.9 %shard_map.103 = (bf16[8,4096]{1,0:T(8,128)(2,1)}, f32[32,128]{1,0:T(8,128)}, bf16[448,128]{1,0:T(8,128)(2,1)}) custom-call(bf16[8,4096]{1,0:T(8,128)(2,1)} %tok_h.1, bf16[8,4096]{1,0:T(8,128)(2,1)} %gout_h.1, bf16[448,128]{1,0:T(8,128)(2,1)} %bitcast.6, bf16[448,128]{1,0:T(8,128)(2,1)} %bitcast.7, bf16[448,128]{1,0:T(8,128)(2,1)} %bitcast.8, ...), custom_call_target="tpu_custom_call" | custom-call | tf_op jit(solution)/shard_map/pallas_call | solution.py:505
  70.5 1.7 %shard_map.104 = (bf16[8,4096]{1,0:T(8,128)(2,1)}, f32[32,128]{1,0:T(8,128)}, bf16[448,128]{1,0:T(8,128)(2,1)}) custom-call(bf16[8,4096]{1,0:T(8,128)(2,1)} %get-tuple-element.9.i0, f32[32,128]{1,0:T(8,128)} %get-tuple-element.10.i1, bf16[448,128]{1,0:T(8,128)(2,1)} %get-tuple-element.11.i2), custom_call_target="tpu_custom_call" | custom-call | tf_op jit(solution)/shard_map/pallas_call | solution.py:518

commit v6 on v5

--- a/solution.py
+++ b/solution.py
@@ -60,7 +60,8 @@
         return lax.rem(v + e, 2)
 
     ys = [(d, e) for d in (2, 1, 3, 0) for e in (1, 0) if d or e]
-    zs = (4, 3, 5, 2, 6, 1, 7)
+    zs = (4, 3, 5, 2, 6, 1, 7, 0)
+    dps = [(d, e) for d in zs for e in (2, 1, 3, 0) if d or e]
     ts = [(d, e, f) for d in (2, 1, 3, 0) for e in (1, 0) for f in (1, 0) if d or e or f]
 
     def ts_dev(d, e, f):
@@ -72,8 +73,8 @@
     def ys_dev(d, e):
         return {YH: yy(d), YL: ee(yl, e)}
 
-    peers = [{Z: zz(d)} for d in zs]
-    peers += [ys_dev(d, e) for d, e in ys] + [ts_dev(*v) for v in ts if v != (0, 1, 0)]
+    peers = [{Z: zz(1)}, {Z: zz(-1)}] + [ys_dev(d, e) for d, e in ys]
+    peers += [{X: xx(d)} for d in (2, 1, 3)] + [{C: 1 - c}]
     loads = [
         (gout_h, gout), (tok_h, tok), (dw_h, w.at[0, z]), (gate_h, gu.at[0, k]),
         (up_h, gu.at[1, k]), (gw_h, w.at[1, z]), (uw_h, w.at[2, z]), (gain_h, gain),
@@ -261,11 +262,11 @@
             ds_[slot, rows].astype(F32) + rd[way, step, rows].astype(F32)
         ).astype(BF)
 
-    def down_next(s):
-        for i in range(2 if s > 1 else 1):
-            for way in range(2):
-                slot = zz(4 - s if way == 0 else s - 4)
-                down_add(way, slot, s - 1, i ^ way)
+    def down_next(s, i):
+        for way in range(2):
+            slot = zz(4 - s if way == 0 else s - 4)
+            down_add(way, slot, s - 1, i ^ way)
+            if s < 4:
                 down_put(way, slot, s, i ^ way)
 
     for way in range(2):
@@ -328,7 +329,9 @@
     norm_part(1)
     norm_part(3)
     norm_core(0)
-    down_next(1)
+    norm_core(1)
+    down_next(1, 0)
+    down_next(2, 1)
     core_wait(1)
     for d in (0, 1, 3):
         gain_part(d)
@@ -342,32 +345,29 @@
     for d, e, f in ts:
         send(g1.at[mine], g1.at[mine], ts_dev(d, e, f), g1sem.at[0], "g1")
 
-    for d in (1, 3, 2):
-        norm_core(d)
+    norm_core(2)
+    norm_core(3)
+    down_next(2, 0)
+    down_next(3, 1)
     norm_x(0)
-    down_next(2)
+    norm_x(1)
     arrived(g1.at[pl.ds(0, 15)], g1sem.at[0])
 
     @pl.when(c == 1)
     def _():
-        g3[z] = jnp.sum(g1[...], axis=0)
-        for d in zs:
-            send(g3.at[z], g3.at[z], {Z: zz(d)}, g3sem.at[0], "g3")
-
-    for d in (1, 3, 2):
-        norm_x(d)
-    down_next(3)
-
-    @pl.when(c == 1)
-    def _():
-        arrived(g3.at[pl.ds(0, 7)], g3sem.at[0])
-        g4[k] = jnp.sum(g3[...], axis=0)
-        for d in (2, 1, 3):
-            send(g4.at[k], g4.at[k], {YH: yy(d)}, g4sem.at[0], "g3")
-
-    for h in range(2):
-        for way in range(2):
-            down_add(way, z, 3, h)
+        g3[z * NY + k] = jnp.sum(g1[...], axis=0)
+        for d, e in dps:
+            send(
+                g3.at[z * NY + k], g3.at[z * NY + k], {Z: zz(d), YH: yy(e)}, g3sem.at[0], "g3"
+            )
+
+    norm_x(2)
+    norm_x(3)
+    down_next(3, 0)
+    down_next(4, 1)
+
+
+    down_next(4, 0)
     outs = [pltpu.make_async_copy(ds_.at[z], dgrad, lsem.at[0])]
     outs[0].start()
 
@@ -397,12 +397,17 @@
 
     @pl.when(c == 1)
     def _():
-        arrived(g4.at[pl.ds(0, 3)], g4sem.at[0])
-        send(g4, g4, core, g4sem.at[1], "g4")
+        arrived(g3.at[pl.ds(0, 31)], g3sem.at[0])
+        for q in range(NY):
+            total = g3[q]
+            for i in range(1, NZ):
+                total = total + g3[i * NY + q]
+            g4[q] = total
+        send(g4, g4, core, g4sem.at[0], "g4")
 
     @pl.when(c == 0)
     def _():
-        arrived(g4, g4sem.at[1])
+        arrived(g4, g4sem.at[0])
 
     for i in range(NZ):
         for q in range(NY):
@@ -414,7 +419,7 @@
         "w0": w.at[0, pl.ds(0, 7)], "w1": w.at[0, pl.ds(0, 7)], "w2": w.at[0, pl.ds(0, 7)],
         "gu": w.at[0, pl.ds(0, 6)], "ga": w.at[0, pl.ds(0, 6)], "down": w.at[0, pl.ds(0, 7)],
         "s1": units(14), "x0": units(56), "x1": units(56), "norm": units(63),
-        "g1": g1.at[pl.ds(0, 15)], "g3": g1.at[pl.ds(0, 10)], "g4": g4,
+        "g1": g1.at[pl.ds(0, 15)], "g3": g3.at[pl.ds(0, 31)], "g4": g4,
     }
 
     def all_sent(late):
@@ -475,7 +480,7 @@
         vm((2, 4, 448, 128), BF),
         vm((8, 1024), F32),
         vm((16, 8, 128), F32),
-        vm((NZ, 8, 128), F32),
+        vm((NZ * NY, 8, 128), F32),
         vm((NY, 8, 128), F32),
         vm((8, 128), F32),
         dma((8,)),
@@ -494,7 +499,7 @@
         dma((2, 4, 2)),
         dma((1,)),
         dma((1,)),
-        dma((2,)),
+        dma((1,)),
     ]
     hbm = pl.BlockSpec(memory_space=pl.ANY)
     shapes = (

time: 72.3 us -> 71.8 us (level)
  no operation moved by 1% of the time
where the time goes in v6:
time: 71.8 us; the launch traced here: 71.6 us
  Pallas kernels  71 us (99%)
    pallas_call x1, Pallas kernels, per_device(): pl.pallas_call(kernel, out_shape=shapes, in_specs=[hbm] * 8, out_specs=(h...  69.3 us
    pallas_call x1, Pallas kernels, per_device(): pl.pallas_call(hand_on, out_shape=shapes, in_specs=[hbm] * 3, out_specs=(...  1.65 us

profile of v6, /device:TPU:1, one launch (start us, length us, event | category | flops | bytes accessed | tf_op | source)
XLA Modules:
  0.0 71.6 jit_solution(11410162093777328230)
XLA Ops:
  0.6 69.3 %shard_map.103 = (bf16[8,4096]{1,0:T(8,128)(2,1)}, f32[32,128]{1,0:T(8,128)}, bf16[448,128]{1,0:T(8,128)(2,1)}) custom-call(bf16[8,4096]{1,0:T(8,128)(2,1)} %tok_h.1, bf16[8,4096]{1,0:T(8,128)(2,1)} %gout_h.1, bf16[448,128]{1,0:T(8,128)(2,1)} %bitcast.6, bf16[448,128]{1,0:T(8,128)(2,1)} %bitcast.7, bf16[448,128]{1,0:T(8,128)(2,1)} %bitcast.8, ...), custom_call_target="tpu_custom_call" | custom-call | tf_op jit(solution)/shard_map/pallas_call | solution.py:510
  70.0 1.7 %shard_map.104 = (bf16[8,4096]{1,0:T(8,128)(2,1)}, f32[32,128]{1,0:T(8,128)}, bf16[448,128]{1,0:T(8,128)(2,1)}) custom-call(bf16[8,4096]{1,0:T(8,128)(2,1)} %get-tuple-element.9.i0, f32[32,128]{1,0:T(8,128)} %get-tuple-element.10.i1, bf16[448,128]{1,0:T(8,128)(2,1)} %get-tuple-element.11.i2), custom_call_target="tpu_custom_call" | custom-call | tf_op jit(solution)/shard_map/pallas_call | solution.py:523

commit v7 on v6

--- a/solution.py
+++ b/solution.py
@@ -182,12 +182,13 @@
     s1_wait(0)
     x_send(0)
     dwr.nxt(2)
-    dwr.nxt(3)
+    dwr.nxt(3, (0,))
     gwr.first()
     uwr.first()
     x_wait(0)
+    dwr.nxt(3, (1,))
     dwr.last()
-    gater.nxt(1)
+    gater.nxt(1, (0,))
     core_wait(0)
 
     down = jnp.concatenate([w[0, i] for i in range(NZ)], axis=1)
@@ -220,17 +221,19 @@
         arrived(rb.at[n], rbsem.at[n])
         sa[2 * n, rows] = (part[n, rows] + rb[n].astype(F32)).astype(BF)
         send(half(sa.at[2 * n], h), half(ra.at[n], h), dev, rasem.at[n], "ga")
-    upr.nxt(1)
+    upr.nxt(1, (0,))
     gwr.nxt(2)
     uwr.nxt(2)
     x_wait(1)
-    gwr.nxt(3)
+    gwr.nxt(3, (0,))
     for n in range(2):
         arrived(ra.at[n], rasem.at[n])
     ga[k] = (part[2] + ra[0].astype(F32) + ra[1].astype(F32)).astype(BF)
     gar.first()
 
+    gater.nxt(1, (1,))
     gater.last()
+    upr.nxt(1, (1,))
     upr.last()
     for j in range(NY):
         gv = gu[0, j].astype(F32)
@@ -240,7 +243,7 @@
         fac[0, j] = uv * sg * (1.0 + gv * (1.0 - sg))
         fac[1, j] = sv
         act[j] = (sv * uv).astype(BF)
-    uwr.nxt(3)
+    uwr.nxt(3, (0,))
 
     acts = jnp.concatenate([act[j] for j in range(NY)], axis=1)
     rows_all = a.at[0].reshape(512, 1024)
@@ -322,7 +325,9 @@
 
     gacc[...] = jnp.zeros((8, 1024), F32)
     gar.nxt(1, (0,))
+    gwr.nxt(3, (1,))
     gwr.last()
+    uwr.nxt(3, (1,))
     uwr.last()
     norm_part(0)
     gar.nxt(1, (1,))
@@ -403,18 +408,15 @@
             for i in range(1, NZ):
                 total = total + g3[i * NY + q]
             g4[q] = total
-        send(g4, g4, core, g4sem.at[0], "g4")
+        send(g4, ggrad, core, g4sem.at[0], "g4")
+        mine = pltpu.make_async_copy(g4, ggrad, lsem.at[2])
+        mine.start()
+        mine.wait()
 
     @pl.when(c == 0)
     def _():
         arrived(g4, g4sem.at[0])
 
-    for i in range(NZ):
-        for q in range(NY):
-            b = i * NY + q
-            gain[b:b + 1, :] = g4[q, i:i + 1, :]
-    outs.append(pltpu.make_async_copy(gain, ggrad, lsem.at[2]))
-    outs[2].start()
     sent = {
         "w0": w.at[0, pl.ds(0, 7)], "w1": w.at[0, pl.ds(0, 7)], "w2": w.at[0, pl.ds(0, 7)],
         "gu": w.at[0, pl.ds(0, 6)], "ga": w.at[0, pl.ds(0, 6)], "down": w.at[0, pl.ds(0, 7)],
@@ -437,14 +439,20 @@
         cp.wait()
 
 
-def hand_on(i0, i1, i2, o0, o1, o2, b0, b1, b2, sem):
+def hand_on(i0, i1, i2, o0, o1, o2, b0, b1, b2, rows, sem):
     ins = [pltpu.make_async_copy(s, d, sem.at[0, n]) for n, (s, d) in enumerate(((i0, b0), (i1, b1), (i2, b2)))]
-    outs = [pltpu.make_async_copy(s, d, sem.at[1, n]) for n, (s, d) in enumerate(((b0, o0), (b1, o1), (b2, o2)))]
+    outs = [pltpu.make_async_copy(s, d, sem.at[1, n]) for n, (s, d) in enumerate(((b0, o0), (rows, o1), (b2, o2)))]
     for cp in ins:
         cp.start()
-    for i, o in zip(ins, outs):
-        i.wait()
-        o.start()
+    ins[1].wait()
+    for i in range(NZ):
+        for q in range(NY):
+            b = i * NY + q
+            rows[b:b + 1, :] = b1[q, i:i + 1, :]
+    outs[1].start()
+    for n in (0, 2):
+        ins[n].wait()
+        outs[n].start()
     for cp in outs:
         cp.wait()
 
@@ -509,7 +517,7 @@
     )
     results = pl.pallas_call(
         kernel,
-        out_shape=shapes,
+        out_shape=(shapes[0], jax.ShapeDtypeStruct((NY, 8, 128), F32), shapes[2]),
         in_specs=[hbm] * 8,
         out_specs=(hbm,) * 3,
         scratch_shapes=scratch,
@@ -525,7 +533,10 @@
         out_shape=shapes,
         in_specs=[hbm] * 3,
         out_specs=(hbm,) * 3,
-        scratch_shapes=[vm(v.shape, v.dtype) for v in shapes] + [dma((2, 3))],
+        scratch_shapes=[
+            vm((8, 4096), BF), vm((NY, 8, 128), F32), vm((448, 128), BF), vm((32, 128), F32),
+            dma((2, 3)),
+        ],
         compiler_params=pltpu.CompilerParams(vmem_limit_bytes=60 * 1024 * 1024),
     )(*results)
     return igrad, ggrad.reshape(4096), dgrad

time: 71.8 us -> 72.2 us (level)
  no operation moved by 1% of the time
where the time goes in v7:
time: 72.2 us; the launch traced here: 72 us
  Pallas kernels  71.3 us (99%)
    pallas_call x1, Pallas kernels, per_device(): pl.pallas_call(kernel, out_shape=(shapes[0], jax.ShapeDtypeStruct((NY, 8,...  69.7 us
    pallas_call x1, Pallas kernels, per_device(): pl.pallas_call(hand_on, out_shape=shapes, in_specs=[hbm] * 3, out_specs=(...  1.65 us

profile of v7, /device:TPU:1, one launch (start us, length us, event | category | flops | bytes accessed | tf_op | source)
XLA Modules:
  0.0 72.0 jit_solution(1547109024103714491)
XLA Ops:
  0.6 69.7 %shard_map.103 = (bf16[8,4096]{1,0:T(8,128)(2,1)}, f32[4,8,128]{2,1,0:T(8,128)}, bf16[448,128]{1,0:T(8,128)(2,1)}) custom-call(bf16[8,4096]{1,0:T(8,128)(2,1)} %tok_h.1, bf16[8,4096]{1,0:T(8,128)(2,1)} %gout_h.1, bf16[448,128]{1,0:T(8,128)(2,1)} %bitcast.6, bf16[448,128]{1,0:T(8,128)(2,1)} %bitcast.7, bf16[448,128]{1,0:T(8,128)(2,1)} %bitcast.8, ...), custom_call_target="tpu_custom_call" | custom-call | tf_op jit(solution)/shard_map/pallas_call | solution.py:518
  70.3 1.7 %shard_map.104 = (bf16[8,4096]{1,0:T(8,128)(2,1)}, f32[32,128]{1,0:T(8,128)}, bf16[448,128]{1,0:T(8,128)(2,1)}) custom-call(bf16[8,4096]{1,0:T(8,128)(2,1)} %get-tuple-element.9.i0, f32[4,8,128]{2,1,0:T(8,128)} %get-tuple-element.10.i1, bf16[448,128]{1,0:T(8,128)(2,1)} %get-tuple-element.11.i2), custom_call_target="tpu_custom_call" | custom-call | tf_op jit(solution)/shard_map/pallas_call | solution.py:531
